TPU v7x, 128 devices: a whole 4x4x4 slice. The times are simulated.
128 devices in a mesh: clip: 8 (over z, core), tm: 16 (over y, x).
Axes of the slice: x: 4, y: 4, z: 4, core: 2. Of those that a mesh axis runs over, the one named last changes fastest.
Arguments:
- tokens: bfloat16 [8, 16, 256, 2048], P('clip', 'tm'), may hold values from -16 to 16
- spatial_queries: bfloat16 [8, 16, 256, 1024], P('clip', 'tm'), may hold values from -4.5 to 4.5
- spatial_keys: bfloat16 [8, 16, 256, 1024], P('clip', 'tm'), may hold values from -4.5 to 4.5
- spatial_values: bfloat16 [8, 16, 256, 1024], P('clip', 'tm'), may hold values from -6 to 6
- spatial_proj: bfloat16 [1024, 2048], P('tm'), may hold values from -0.1875 to 0.1875
- temporal_qkv: bfloat16 [2048, 3072], P('tm'), may hold values from -0.13258252 to 0.13258252
- temporal_proj: bfloat16 [1024, 2048], P('tm'), may hold values from -0.1875 to 0.1875
- frame_mask: int32 [8, 16, 16], P('clip'), may hold values from 0 to 1, as said below
- expert_ids: int32 [8, 16, 256, 2], P('clip', 'tm'), may hold values from 0 to 127, all different within a row; in each aligned block of 256 rows (0 to 255, 256 to 511, ..., all dimensions but the last counted through in order) at most 8 rows name the same one
- gate_values: float32 [8, 16, 256, 2], P('clip', 'tm'), may hold values from 0.2 to 1
- expert_gate: bfloat16 [128, 2048, 1408], P(('clip', 'tm')), may hold values from -0.125 to 0.125
- expert_up: bfloat16 [128, 2048, 1408], P(('clip', 'tm')), may hold values from -0.125 to 0.125
- expert_down: bfloat16 [128, 1408, 2048], P(('clip', 'tm')), may hold values from -0.15625 to 0.15625
Outputs:
- layer_out: bfloat16 [8, 16, 256, 2048], P('clip', 'tm')
Inputs may be any that keep to these rules, and one draw needn't show every extreme that they name: `expert_ids`: each token names 2 different experts. Among the 256 tokens of one clip and frame, no expert is named by more than 8 tokens, and in some frames one expert is named by exactly 8. frame_mask[c, i, j] is 1 where j = i and 0 where j > i.
All inputs are finite; a program needn't handle non-finite values.
Results may differ from a plain program's by a relative error of at most 0.013.
Values may be sent and summed in bfloat16 or wider, within the bound.
A program may use at most 128 MiB of HBM per device.

v0:
```python
import math

import jax
import jax.numpy as jnp
from jax import lax
from jax.sharding import PartitionSpec as P

HEADS = 8
HD = 128
TOP = 2


EPS = 1e-06
MASKED = -1e30


def grouped_exchange(x, axis, split_dim, concat_dim, work, item_dim, out_dim):

    def moved(group):
        return lax.all_to_all(group, axis, split_axis=split_dim, concat_axis=concat_dim, tiled=True)

    items = jax.tree.leaves(x)[0].shape[item_dim]
    ends = [items * k // 2 for k in range(2 + 1)] if items % 2 == 0 else [0, items]
    groups = [
        jax.tree.map(lambda a: lax.slice_in_dim(a, low, high, axis=item_dim), x)
        for low, high in zip(ends, ends[1:])
    ]
    arrived = [moved(group) for group in groups]
    made = [work(group) for group in arrived]
    return jax.tree.map(lambda *parts: jnp.concatenate(parts, axis=out_dim), *made)


def rms_normed(values):
    wide = values.astype(jnp.float32)
    inverse = lax.rsqrt(jnp.mean(wide * wide, axis=-1, keepdims=True) + EPS)
    return (wide * inverse).astype(jnp.bfloat16)


def normalize_rows(scores):
    row_max = jnp.max(scores, axis=-1, keepdims=True)
    exp_terms = jnp.exp(scores - row_max)
    return (exp_terms / jnp.sum(exp_terms, axis=-1, keepdims=True)).astype(jnp.bfloat16)


def add_columns(left_side, piece):
    return jnp.dot(left_side, piece, preferred_element_type=jnp.float32)


def spatial_mix(queries, keys, values):
    positions = queries.shape[0]
    score_scale = 1.0 / math.sqrt(HD)
    query_heads = queries.reshape(positions, HEADS, HD)
    key_heads = keys.reshape(positions, HEADS, HD)
    value_heads = values.reshape(positions, HEADS, HD)
    scores = (
        jnp.einsum("qhd,khd->hqk", query_heads, key_heads, preferred_element_type=jnp.float32)
        * score_scale
    )
    weights = normalize_rows(scores)
    mixed = jnp.einsum("hqk,khd->qhd", weights, value_heads, preferred_element_type=jnp.float32)
    return mixed.astype(jnp.bfloat16).reshape(positions, HEADS * HD)


def temporal_mix(queries, keys, values, allowed):
    frames, positions = (queries.shape[0], queries.shape[1])
    score_scale = 1.0 / math.sqrt(HD)
    query_heads = queries.reshape(frames, positions, HEADS, HD)
    key_heads = keys.reshape(frames, positions, HEADS, HD)
    value_heads = values.reshape(frames, positions, HEADS, HD)
    scores = (
        jnp.einsum("iphd,jphd->phij", query_heads, key_heads, preferred_element_type=jnp.float32)
        * score_scale
    )
    weights = normalize_rows(jnp.where(allowed[None, None, :, :], scores, MASKED))
    mixed = jnp.einsum("phij,jphd->iphd", weights, value_heads, preferred_element_type=jnp.float32)
    return mixed.astype(jnp.bfloat16).reshape(frames, positions, HEADS * HD)


def temporal_inputs(normed, qkv_rows):
    zero_start = jnp.zeros((normed.shape[0], qkv_rows.shape[1]), jnp.float32)

    def fold_rows(total, piece, start):
        return add_columns(normed, piece)

    return fold_rows(
        zero_start, lax.all_gather(qkv_rows, "tm", axis=0, tiled=True), jnp.int32(0)
    ).astype(jnp.bfloat16)


def temporal_output(mixed, proj_rows):
    zero_start = jnp.zeros((mixed.shape[0], proj_rows.shape[1]), jnp.float32)

    def fold_rows(total, piece, start):
        return add_columns(mixed, piece)

    return fold_rows(
        zero_start, lax.all_gather(proj_rows, "tm", axis=0, tiled=True), jnp.int32(0)
    ).astype(jnp.bfloat16)


def shards(
    tokens,
    spatial_queries,
    spatial_keys,
    spatial_values,
    spatial_proj,
    temporal_qkv,
    temporal_proj,
    frame_mask,
    expert_ids,
    gate_values,
    expert_gate,
    expert_up,
    expert_down,
):
    model_width = tokens.shape[3]
    positions = tokens.shape[2]
    tm_count = lax.axis_size("tm")
    clip_count = lax.axis_size("clip")
    experts = clip_count * tm_count
    per_block = positions // tm_count
    resident = tokens.reshape(positions, model_width)
    attended_space = spatial_mix(
        spatial_queries.reshape(positions, -1),
        spatial_keys.reshape(positions, -1),
        spatial_values.reshape(positions, -1),
    )
    spatial_update = add_columns(
        attended_space, lax.all_gather(spatial_proj, "tm", axis=0, tiled=True)
    )
    first = (resident.astype(jnp.float32) + spatial_update).astype(jnp.bfloat16)
    normed = rms_normed(first)
    allowed = frame_mask[0] == 1
    projected = temporal_inputs(normed, temporal_qkv)
    head_width = projected.shape[1] // 3
    blocks = projected.reshape(tm_count, per_block, 3 * head_width)
    attended_time = temporal_mix(
        lax.all_to_all(blocks[:, :, :head_width], "tm", split_axis=0, concat_axis=0, tiled=True),
        lax.all_to_all(
            blocks[:, :, head_width : 2 * head_width], "tm", split_axis=0, concat_axis=0, tiled=True
        ),
        lax.all_to_all(
            blocks[:, :, 2 * head_width :], "tm", split_axis=0, concat_axis=0, tiled=True
        ),
        allowed,
    )
    mixed_back = lax.all_to_all(attended_time, "tm", split_axis=0, concat_axis=0, tiled=True)
    temporal_update = temporal_output(mixed_back.reshape(positions, head_width), temporal_proj)
    second = (first.astype(jnp.float32) + temporal_update.astype(jnp.float32)).astype(jnp.bfloat16)
    routed = rms_normed(second)
    capacity = 2 * TOP * positions // experts
    slot_count = experts * capacity
    pair_ids = expert_ids.reshape(positions * TOP)
    chosen = (pair_ids[:, None] == jnp.arange(experts, dtype=jnp.int32)[None, :]).astype(jnp.int32)
    earlier = jnp.cumsum(chosen, axis=0) - chosen
    pair_rank = jnp.sum(earlier * chosen, axis=1)
    pair_slot = pair_ids * capacity + pair_rank
    slot_index = jnp.arange(slot_count, dtype=jnp.int32)
    pair_onehot = (pair_slot[:, None] == slot_index[None, :]).astype(jnp.bfloat16)
    token_onehot = jnp.any(
        pair_slot.reshape(positions, TOP)[:, :, None] == slot_index[None, None, :], axis=1
    ).astype(jnp.bfloat16)
    outgoing = lax.dot_general(
        token_onehot, routed, (((0,), (0,)), ((), ())), preferred_element_type=jnp.float32
    )
    outgoing = outgoing.astype(jnp.bfloat16).reshape(experts, capacity, model_width)

    def expert_rows(received):
        flat_rows = received.reshape(-1, model_width)
        gate_part = jnp.dot(flat_rows, expert_gate[0], preferred_element_type=jnp.float32)
        up_part = jnp.dot(flat_rows, expert_up[0], preferred_element_type=jnp.float32)
        hidden = (jax.nn.silu(gate_part) * up_part).astype(jnp.bfloat16)
        answer = jnp.dot(hidden, expert_down[0], preferred_element_type=jnp.float32).astype(
            jnp.bfloat16
        )
        return answer.reshape(received.shape)

    def serve_slots(received):
        return lax.all_to_all(
            expert_rows(received), ("clip", "tm"), split_axis=0, concat_axis=0, tiled=True
        )

    answers = grouped_exchange(outgoing, ("clip", "tm"), 0, 0, serve_slots, 1, 1)
    pair_answers = jnp.dot(
        pair_onehot, answers.reshape(slot_count, model_width), preferred_element_type=jnp.float32
    )
    weighted = pair_answers.reshape(positions, TOP, model_width) * gate_values.reshape(
        positions, TOP, 1
    )
    expert_mix = jnp.sum(weighted, axis=1)
    layer_out = (second.astype(jnp.float32) + expert_mix).astype(jnp.bfloat16)
    return layer_out.reshape(tokens.shape)


def solution(mesh):
    placed = (
        P("clip", "tm", None, None),
        P("clip", "tm", None, None),
        P("clip", "tm", None, None),
        P("clip", "tm", None, None),
        P("tm", None),
        P("tm", None),
        P("tm", None),
        P("clip", None, None),
        P("clip", "tm", None, None),
        P("clip", "tm", None, None),
        P(("clip", "tm"), None, None),
        P(("clip", "tm"), None, None),
        P(("clip", "tm"), None, None),
    )
    return jax.shard_map(
        shards, mesh=mesh, in_specs=placed, out_specs=P("clip", "tm", None, None), check_vma=False
    )
```

profile of v0, /device:TPU:1, one launch (start us, length us, event | category | flops | bytes accessed | tf_op | source)
XLA Modules:
  0.0 404.5 jit_solution(15709325353586606955)
XLA Ops:
  10.2 2.1 fusion.92
  12.3 2.0 convolution_convert_fusion.3
  14.3 49.5 %all-gather.4.cloned.1.call-done = bf16[1024,2048]{1,0:T(8,128)(2,1)} async-done(((bf16[64,2048]{1,0:T(8,128)(2,1)}), bf16[1024,2048]{1,0:T(8,128)(2,1)}) %all-gather.4.cloned.1.call-update) | async-done | bytes 4194320 | tf_op jit(solution)/shard_map/all_gather | solution.py:129
  63.8 3.6 fusion.38
  67.4 87.9 %all-gather.6.cloned.1.call-done = bf16[2048,3072]{1,0:T(8,128)(2,1)} async-done(((bf16[128,3072]{1,0:T(8,128)(2,1)}), bf16[2048,3072]{1,0:T(8,128)(2,1)}) %all-gather.6.cloned.1.call-update) | async-done | bytes 12582928 | tf_op jit(solution)/shard_map/all_gather | solution.py:86
  155.3 8.1 %convolution_convert_fusion = bf16[256,3072]{1,0:T(8,128)(2,1)S(1)} fusion(bf16[2048,3072]{1,0:T(8,128)(2,1)} %all-gather.6.cloned.1.call-done, bf16[256,2048]{1,0:T(8,128)(2,1)S(1)} %get-tuple-element.13, f32[256]{0:T(256)S(1)} %add_rsqrt_fusion.1), kind=kOutput, calls=%fused_computation.20 | convolution fusion | flops 3223584768 | bytes 15205376 | tf_op jit(solution)/shard_map/dot_general | solution.py:46
  164.6 17.8 %all_to_all.40 = bf16[16,16,1024]{2,1,0:T(8,128)(2,1)S(1)} all-to-all(bf16[16,16,1024]{2,1,0:T(8,128)(2,1)S(1)} %get-tuple-element.9), channel_id=1, replica_groups=mesh['clip'=8,'tm'=16] {'tm'}, dimensions={0} | all-to-all | bytes 1048576 | tf_op jit(solution)/shard_map/all_to_all | solution.py:138
  182.4 3.6 all-to-all-start.2
  186.6 9.0 %all-to-all-done.2 = bf16[16,16,1024]{2,1,0:T(8,128)(2,1)S(1)} async-done(((bf16[16,16,1024]{2,1,0:T(8,128)(2,1)}), bf16[16,16,1024]{2,1,0:T(8,128)(2,1)S(1)}, u32[]{:S(2)}, u32[]{:S(2)}) %all-to-all-start.2) | async-done | bytes 524320 | tf_op jit(solution)/shard_map/all_to_all | solution.py:139
  195.6 3.6 all-to-all-start
  199.7 15.8 %all-to-all-done = bf16[16,16,1024]{2,1,0:T(8,128)(2,1)S(1)} async-done(((bf16[16,16,1024]{2,1,0:T(8,128)(2,1)}), bf16[16,16,1024]{2,1,0:T(8,128)(2,1)S(1)}, u32[]{:S(2)}, u32[]{:S(2)}) %all-to-all-start) | async-done | bytes 524320 | tf_op jit(solution)/shard_map/all_to_all | solution.py:142
  215.7 1.7 fusion.97
  217.3 1.3 fusion.50
  219.9 3.8 all-to-all-start.3
  224.4 8.3 %all-to-all-done.3 = bf16[16,16,1024]{2,1,0:T(8,128)(2,1)S(1)} async-done(((bf16[16,16,1024]{2,1,0:T(8,128)(2,1)}), bf16[16,16,1024]{2,1,0:T(8,128)(2,1)S(1)}, u32[]{:S(2)}, u32[]{:S(2)}) %all-to-all-start.3) | async-done | bytes 524320 | tf_op jit(solution)/shard_map/all_to_all | solution.py:147
  232.7 3.9 fusion.40
  236.6 1.4 convert_bitcast_fusion
  238.0 3.3 fusion.90
  241.3 39.5 %all_to_all.41 = bf16[128,4,2048]{2,1,0:T(4,128)(2,1)} all-to-all(bf16[128,4,2048]{2,1,0:T(4,128)(2,1)S(1)} %get-tuple-element.5), channel_id=1, replica_groups=mesh['clip'=8,'tm'=16] {'clip','tm'}, dimensions={0} | all-to-all | bytes 4194304 | tf_op jit(solution)/shard_map/all_to_all | solution.py:20
  280.8 4.8 %all-to-all-start.6 = ((bf16[128,4,2048]{2,1,0:T(4,128)(2,1)}), bf16[128,4,2048]{2,1,0:T(4,128)(2,1)S(1)}, u32[]{:S(2)}, u32[]{:S(2)}) async-start(bf16[128,4,2048]{2,1,0:T(4,128)(2,1)} %get-tuple-element.6), calls=%async_computation.6 | async-start | bytes 4194304 | tf_op jit(solution)/shard_map/all_to_all | solution.py:20
  285.6 4.0 reshape.146
  289.6 8.3 %fusion.12 = f32[512,1408]{1,0:T(8,128)} fusion(bf16[512,2048]{1,0:T(8,128)(2,1)} %reshape.146, bf16[1,2048,1408]{2,1,0:T(8,128)(2,1)} %param.23), kind=kOutput, calls=%fused_computation.12 | convolution fusion | flops 2952790016 | bytes 10747904 | tf_op jit(solution)/shard_map/dot_general | solution.py:170
  297.8 13.9 %fusion.29 = bf16[512,2048]{1,0:T(8,128)(2,1)} fusion(bf16[1,1408,2048]{2,1,0:T(8,128)(2,1)} %param.25, bf16[512,2048]{1,0:T(8,128)(2,1)} %reshape.146, bf16[1,2048,1408]{2,1,0:T(8,128)(2,1)} %param.24, f32[512,1408]{1,0:T(8,128)} %fusion.12), kind=kOutput, calls=%fused_computation.31 | convolution fusion | flops 5910953984 | bytes 18612224 | tf_op jit(solution)/shard_map/dot_general | solution.py:173
  311.7 4.1 %reshape.147 = bf16[128,4,2048]{2,1,0:T(4,128)(2,1)} reshape(bf16[512,2048]{1,0:T(8,128)(2,1)} %fusion.29) | data formatting | bytes 4194304 | tf_op jit(solution)/shard_map/reshape | solution.py:176
  315.8 10.2 %all-to-all-start.5 = ((bf16[128,4,2048]{2,1,0:T(4,128)(2,1)}), bf16[128,4,2048]{2,1,0:T(4,128)(2,1)}, u32[]{:S(2)}, u32[]{:S(2)}) async-start(bf16[128,4,2048]{2,1,0:T(4,128)(2,1)} %reshape.147), calls=%async_computation.5 | async-start | bytes 4194304 | tf_op jit(solution)/shard_map/all_to_all | solution.py:179
  326.1 2.1 reshape.148
  328.1 8.4 %fusion.10 = f32[512,1408]{1,0:T(8,128)} fusion(bf16[512,2048]{1,0:T(8,128)(2,1)} %reshape.148, bf16[1,2048,1408]{2,1,0:T(8,128)(2,1)} %param.23), kind=kOutput, calls=%fused_computation.10 | convolution fusion | flops 2952790016 | bytes 10747904 | tf_op jit(solution)/shard_map/dot_general | solution.py:170
  336.5 13.3 %fusion.32 = bf16[512,2048]{1,0:T(8,128)(2,1)} fusion(bf16[1,1408,2048]{2,1,0:T(8,128)(2,1)} %param.25, bf16[512,2048]{1,0:T(8,128)(2,1)S(1)} %copy-done, bf16[1,2048,1408]{2,1,0:T(8,128)(2,1)} %param.24, f32[512,1408]{1,0:T(8,128)} %fusion.10), kind=kOutput, calls=%fused_computation.32 | convolution fusion | flops 5910953984 | bytes 18612224 | tf_op jit(solution)/shard_map/dot_general | solution.py:173
  349.8 2.7 reshape.149
  352.6 2.8 all-to-all-done.5
  355.4 36.4 %all_to_all.42 = bf16[128,4,2048]{2,1,0:T(4,128)(2,1)S(1)} all-to-all(bf16[128,4,2048]{2,1,0:T(4,128)(2,1)S(1)} %reshape.149), channel_id=1, replica_groups=mesh['clip'=8,'tm'=16] {'clip','tm'}, dimensions={0} | all-to-all | bytes 4194304 | tf_op jit(solution)/shard_map/all_to_all | solution.py:179
  391.8 4.8 %multiply_reduce_fusion = f32[256,2048]{1,0:T(8,128)S(1)} fusion(bf16[128,4,2048]{2,1,0:T(4,128)(2,1)S(1)} %all_to_all.42, bf16[128,4,2048]{2,1,0:T(4,128)(2,1)} %all-to-all-done.5, f32[256,2]{0,1:T(2,128)S(1)} %bitcast.127, s32[256,2]{0,1:T(2,128)S(1)} %copy.52), kind=kOutput, calls=%fused_computation.18 | convolution fusion | flops 2157969408 | bytes 6295552 | tf_op jit(solution)/shard_map/dot_general | solution.py:184
  (54 shorter events, 9.2 us)
Async XLA Ops:
  6.5 3.4 copy-start.1
  6.5 3.5 copy-start.2
  6.5 57.3 %all-gather.4.cloned.1.call-start = ((), (), s32[]{:S(2)}) async-start(), calls=%async_computation.8 | async-start | bytes 4456448 | tf_op jit(solution)/shard_map/all_gather | solution.py:129
  7.3 148.1 %all-gather.6.cloned.1.call-start = ((), (), s32[]{:S(2)}) async-start(), calls=%async_computation.9 | async-start | bytes 13369344 | tf_op jit(solution)/shard_map/all_gather | solution.py:86
  8.0 216.4 %all-gather.8.cloned.1.call-start = ((), (), s32[]{:S(2)}) async-start(), calls=%async_computation.10 | async-start | bytes 4456448 | tf_op jit(solution)/shard_map/all_gather | solution.py:97
  12.3 51.5 %copy-start.5 = (bf16[1,1,256,2048]{3,2,1,0:T(8,128)(2,1)S(1)}, bf16[1,1,256,2048]{3,2,1,0:T(8,128)(2,1)}, u32[]{:S(2)}) copy-start(bf16[1,1,256,2048]{3,2,1,0:T(8,128)(2,1)} %param.13) | copy-start | bytes 3145732
  67.4 96.1 %copy-start.7 = (bf16[256,2048]{1,0:T(8,128)(2,1)}, bf16[256,2048]{1,0:T(8,128)(2,1)S(1)}, u32[]{:S(2)}) copy-start(bf16[256,2048]{1,0:T(8,128)(2,1)S(1)} %get-tuple-element.13) | copy-start | bytes 3145732
  163.5 22.5 %copy-start.4 = (s32[1,1,256,2]{2,3,1,0:T(2,128)S(1)}, s32[1,1,256,2]{2,3,1,0:T(2,128)}, u32[]{:S(2)}) copy-start(s32[1,1,256,2]{2,3,1,0:T(2,128)} %param.21) | copy-start | bytes 6148
  164.6 34.6 %copy-start.3 = (s32[1,16,16]{2,1,0:T(8,128)S(1)}, s32[1,16,16]{2,1,0:T(8,128)}, u32[]{:S(2)}) copy-start(s32[1,16,16]{2,1,0:T(8,128)} %param.20) | copy-start | bytes 3076
  182.4 13.2 %all-to-all-start.2 = ((bf16[16,16,1024]{2,1,0:T(8,128)(2,1)}), bf16[16,16,1024]{2,1,0:T(8,128)(2,1)S(1)}, u32[]{:S(2)}, u32[]{:S(2)}) async-start(bf16[16,16,1024]{2,1,0:T(8,128)(2,1)} %get-tuple-element.8), calls=%async_computation.2 | async-start | bytes 1048576 | tf_op jit(solution)/shard_map/all_to_all | solution.py:139
  195.6 20.0 %all-to-all-start = ((bf16[16,16,1024]{2,1,0:T(8,128)(2,1)}), bf16[16,16,1024]{2,1,0:T(8,128)(2,1)S(1)}, u32[]{:S(2)}, u32[]{:S(2)}) async-start(bf16[16,16,1024]{2,1,0:T(8,128)(2,1)} %get-tuple-element.7), calls=%async_computation | async-start | bytes 1048576 | tf_op jit(solution)/shard_map/all_to_all | solution.py:142
  219.9 12.8 %all-to-all-start.3 = ((bf16[16,16,1024]{2,1,0:T(8,128)(2,1)}), bf16[16,16,1024]{2,1,0:T(8,128)(2,1)S(1)}, u32[]{:S(2)}, u32[]{:S(2)}) async-start(bf16[16,16,1024]{2,1,0:T(8,128)(2,1)} %reshape.142), calls=%async_computation.3 | async-start | bytes 1048576 | tf_op jit(solution)/shard_map/all_to_all | solution.py:147
  280.8 35.0 %all-to-all-start.6 = ((bf16[128,4,2048]{2,1,0:T(4,128)(2,1)}), bf16[128,4,2048]{2,1,0:T(4,128)(2,1)S(1)}, u32[]{:S(2)}, u32[]{:S(2)}) async-start(bf16[128,4,2048]{2,1,0:T(4,128)(2,1)} %get-tuple-element.6), calls=%async_computation.6 | async-start | bytes 4194304 | tf_op jit(solution)/shard_map/all_to_all | solution.py:20
  315.8 39.6 %all-to-all-start.5 = ((bf16[128,4,2048]{2,1,0:T(4,128)(2,1)}), bf16[128,4,2048]{2,1,0:T(4,128)(2,1)}, u32[]{:S(2)}, u32[]{:S(2)}) async-start(bf16[128,4,2048]{2,1,0:T(4,128)(2,1)} %reshape.147), calls=%async_computation.5 | async-start | bytes 4194304 | tf_op jit(solution)/shard_map/all_to_all | solution.py:179
  328.1 8.4 %copy-start = (bf16[512,2048]{1,0:T(8,128)(2,1)S(1)}, bf16[512,2048]{1,0:T(8,128)(2,1)}, u32[]{:S(2)}) copy-start(bf16[512,2048]{1,0:T(8,128)(2,1)} %reshape.148) | copy-start | bytes 6291460
  352.6 39.3 %copy-start.6 = (f32[1,1,256,2]{2,3,1,0:T(2,128)S(1)}, f32[1,1,256,2]{2,3,1,0:T(2,128)}, u32[]{:S(2)}) copy-start(f32[1,1,256,2]{2,3,1,0:T(2,128)} %param.22) | copy-start | bytes 6148
Sparse Core Ops, SparseCore 0:
  9.5 54.2 all-gather.3
  66.0 89.3 all-gather.5
  157.5 62.4 all-gather.7
where the time goes:
time: 406 us; the launch traced here: 404 us
  waiting for transfers between devices  175 us (43%)
  blocking collectives  93.8 us (23%)
  matrix products  72.7 us (18%)
  starting transfers between devices  26 us (6%)
  local copies, waits for them, and re-layouts  21.1 us (5%)
  between operations  13.4 us (3%)
    all_gather x1, waiting for transfers between devices, temporal_inputs(): lax.all_gather(qkv_rows, 'tm', axis=0, tiled=True)  87.9 us
    all_gather x1, waiting for transfers between devices, shards(): lax.all_gather(spatial_proj, 'tm', axis=0, tiled=True)  49.5 us
    all_to_all x1, blocking collectives, moved(): lax.all_to_all(group, axis, split_axis=split_dim, concat_axis=concat_dim,...  39.5 us
    all_to_all x1, blocking collectives, serve_slots(): lax.all_to_all(expert_rows(received), ('clip', 'tm'), split_axis=0, conca...  36.4 us
    dot_general x2, matrix products, expert_rows(): jnp.dot(hidden, expert_down[0], preferred_element_type=jnp.float32)  27.2 us
    all_to_all x1, blocking collectives, shards(): lax.all_to_all(blocks[:, :, :head_width], 'tm', split_axis=0, concat_axis...  17.8 us
    dot_general x2, matrix products, expert_rows(): jnp.dot(flat_rows, expert_gate[0], preferred_element_type=jnp.float32)  16.6 us
    all_to_all x1, waiting for transfers between devices, shards(): lax.all_to_all(blocks[:, :, 2 * head_width:], 'tm', split_axis=0, concat_...  15.8 us
  transfers between devices with their start and end apart: 8, of which 6 were waited for; matrix products, arithmetic and copies ran while one was open for 20% of the time, Pallas kernels for 0%

commit v1 on v0

v1 whole, which is shorter than its diff:
```python
import functools
import math

import jax
import jax.numpy as jnp
from jax import lax
from jax.experimental import pallas as pl
from jax.experimental.pallas import tpu as pltpu
from jax.sharding import PartitionSpec as P

HEADS = 8
HD = 128
TOP = 2
SIDE = 4
TM = 16


EPS = 1e-06
MASKED = -1e30
MESH = pl.DeviceIdType.MESH


def grouped_exchange(x, axis, split_dim, concat_dim, work, item_dim, out_dim):

    def moved(group):
        return lax.all_to_all(group, axis, split_axis=split_dim, concat_axis=concat_dim, tiled=True)

    items = jax.tree.leaves(x)[0].shape[item_dim]
    ends = [items * k // 2 for k in range(2 + 1)] if items % 2 == 0 else [0, items]
    groups = [
        jax.tree.map(lambda a: lax.slice_in_dim(a, low, high, axis=item_dim), x)
        for low, high in zip(ends, ends[1:])
    ]
    arrived = [moved(group) for group in groups]
    made = [work(group) for group in arrived]
    return jax.tree.map(lambda *parts: jnp.concatenate(parts, axis=out_dim), *made)


class Gather:
    def __init__(self, shard, full, place, send, recv):
        self.shard, self.full, self.send, self.recv = shard, full, send, recv
        self.rows = full.shape[1]
        self.place = place

    def part(self, index, quarter=None):
        half = self.rows // 2
        if quarter is None:
            start = pl.multiple_of(self.place["core"] * half, half)
            return self.full.at[index, pl.ds(start, half)]
        size = half // 2
        start = pl.multiple_of(self.place["core"] * half + quarter * size, size)
        return self.full.at[index, pl.ds(start, size)]

    def own_part(self):
        half = self.rows // 2
        start = pl.multiple_of(self.place["core"] * half, half)
        return self.shard.at[pl.ds(start, half)]

    def at(self, step1, step2):
        p = self.place
        return lax.rem(p["i1"] + step1 + SIDE, SIDE) * p["s1"] + lax.rem(p["i2"] + step2 + SIDE, SIDE) * p["s2"]

    def copy(self, src, dst, slot, clip, tm):
        pltpu.make_async_remote_copy(
            src_ref=src,
            dst_ref=dst,
            send_sem=self.send,
            recv_sem=self.recv.at[slot],
            device_id=(clip, tm),
            device_id_type=MESH,
        ).start()

    def arrived(self, ref, slot):
        pltpu.make_async_copy(ref, ref, self.recv.at[slot]).wait()

    def along(self, dim, way, src, dst, slot):
        target = self.at(way, 0) if dim == 1 else self.at(0, way)
        self.copy(src, dst, slot, self.place["clip"], target)

    def push(self, src, dst):
        self.copy(src, dst, 20, self.place["partner"], self.place["tm"])

    OFFSETS = (0, -1, 1, 2)

    def second_dim(self, k):
        index = self.at(self.OFFSETS[k], 0)
        src = self.own_part() if k == 0 else self.part(index)
        self.along(2, 1, src, self.part(index), 4 + 2 * k)
        self.along(2, -1, src, self.part(index), 5 + 2 * k)
        if k > 0:
            self.push(self.part(index), self.part(index))

    def own(self):
        mine = self.part(self.place["tm"])
        self.along(1, 1, self.own_part(), mine, 0)
        self.along(1, -1, self.own_part(), mine, 1)
        self.second_dim(0)

    def first_near(self):
        low, high = self.at(-1, 0), self.at(1, 0)
        self.arrived(self.part(low), 0)
        self.along(1, 1, self.part(low, 0), self.part(low, 0), 2)
        self.second_dim(1)
        self.arrived(self.part(high), 1)
        self.along(1, -1, self.part(high, 1), self.part(high, 1), 3)
        self.second_dim(2)

    def first_far(self):
        far = self.at(2, 0)
        self.arrived(self.part(far, 0), 2)
        self.arrived(self.part(far, 1), 3)
        self.second_dim(3)

    def second_near(self, k):
        step = self.OFFSETS[k]
        low, high = self.at(step, -1), self.at(step, 1)
        self.arrived(self.part(low), 4 + 2 * k)
        self.along(2, 1, self.part(low, 0), self.part(low, 0), 12 + 2 * k)
        self.push(self.part(low), self.part(low))
        self.arrived(self.part(high), 5 + 2 * k)
        self.along(2, -1, self.part(high, 1), self.part(high, 1), 13 + 2 * k)
        self.push(self.part(high), self.part(high))

    def second_far(self, k):
        far = self.at(self.OFFSETS[k], 2)
        self.arrived(self.part(far, 0), 12 + 2 * k)
        self.arrived(self.part(far, 1), 13 + 2 * k)
        self.push(self.part(far), self.part(far))

    def pushed(self):
        half = self.rows // 2
        ref = self.full.at[pl.ds(0, TM - 1), pl.ds(0, half)]
        self.arrived(ref, 20)

    def drained(self):
        ref = self.full.at[pl.ds(0, TM - 1)]
        pltpu.make_async_copy(ref, ref, self.send).wait()


def normed_rows(ref, out):
    def step(block, carry):
        rows = pl.ds(pl.multiple_of(block * 32, 32), 32)
        wide = ref[rows, :].astype(jnp.float32)
        inverse = lax.rsqrt(jnp.mean(wide * wide, axis=-1, keepdims=True) + EPS)
        out[rows, :] = (wide * inverse).astype(jnp.bfloat16)
        return carry

    lax.fori_loop(0, ref.shape[0] // 32, step, 0)


def attend(queries, keys, values, out, bias, heads):
    scale = 1.0 / math.sqrt(HD)

    def step(index, carry):
        for head in (2 * index, 2 * index + 1):
            cols = pl.ds(pl.multiple_of(head * HD, HD), HD)
            scores = lax.dot_general(
                queries[:, cols], keys[:, cols], (((1,), (1,)), ((), ())), preferred_element_type=jnp.float32
            )
            scores = scores * scale
            if bias is not None:
                scores = jnp.where(bias[...] > 0.5, scores, MASKED)
            top = jnp.max(scores, axis=-1, keepdims=True)
            terms = jnp.exp(scores - top)
            weights = (terms * (1.0 / jnp.sum(terms, axis=-1, keepdims=True))).astype(jnp.bfloat16)
            mixed = jnp.dot(weights, values[:, cols], preferred_element_type=jnp.float32)
            out[:, cols] = mixed.astype(jnp.bfloat16)
        return carry

    lax.fori_loop(0, heads // 2, step, 0)


def trunk_kernel(
    tokens, sq, sk, sv, sproj, tqkv, tproj, mask,
    second_out, routed_out,
    tok_v, q_v, k_v, v_v, mixed_v, first_v, normed_v, spread_v, qkv_v, home_v, allowed_v, mask_v,
    wide_v, proj_s, qkv_w, proj_t,
    local_sem, send_sem, recv_s, recv_q, recv_t, swap_send, swap_recv, out_sem,
):
    clip = lax.axis_index("clip")
    tm = lax.axis_index("tm")
    core = lax.rem(clip, 2)
    y, x = tm // SIDE, lax.rem(tm, SIDE)
    positions = tok_v.shape[0]
    per = positions // TM
    place = {
        "clip": clip,
        "tm": tm,
        "core": core,
        "partner": clip + 1 - 2 * core,
        "i1": x * (1 - core) + y * core,
        "i2": y * (1 - core) + x * core,
        "s1": 1 + 3 * core,
        "s2": 4 - 3 * core,
    }
    spatial = Gather(sproj, proj_s, place, send_sem.at[0], recv_s)
    qkv = Gather(tqkv, qkv_w, place, send_sem.at[1], recv_q)
    temporal = Gather(tproj, proj_t, place, send_sem.at[2], recv_t)

    loads = [
        pltpu.make_async_copy(src, dst, local_sem.at[n])
        for n, (src, dst) in enumerate(
            [
                (sq, q_v), (sk, k_v), (sv, v_v), (tokens, tok_v),
                (sproj, proj_s.at[tm]), (tqkv, qkv_w.at[tm]), (tproj, proj_t.at[tm]), (mask, mask_v),
            ]
        )
    ]
    for load in loads:
        load.start()

    barrier = pltpu.get_barrier_semaphore()

    def greet(step, carry):
        pl.semaphore_signal(
            barrier, inc=1, device_id=(clip, lax.rem(tm + step, TM)), device_id_type=MESH
        )
        return carry

    lax.fori_loop(1, TM, greet, 0)
    pl.semaphore_signal(barrier, inc=1, device_id=(place["partner"], tm), device_id_type=MESH)
    pl.semaphore_wait(barrier, TM)

    spatial.own()
    qkv.own()

    for n in (0, 1, 2):
        loads[n].wait()
    attend(q_v, k_v, v_v, mixed_v, None, HEADS)

    spatial.first_near()
    spatial.first_far()
    qkv.first_near()
    temporal.own()
    for k in range(4):
        spatial.second_near(k)
    for k in range(4):
        spatial.second_far(k)
    qkv.first_far()
    loads[3].wait()
    loads[4].wait()
    spatial.pushed()

    model = tok_v.shape[1]
    width = 512

    def project(chunk, carry):
        cols = pl.ds(pl.multiple_of(chunk * width, width), width)
        weights = proj_s[:, :, cols].reshape(mixed_v.shape[1], width)
        update = jnp.dot(mixed_v[...], weights, preferred_element_type=jnp.float32)
        first_v[:, cols] = (tok_v[:, cols].astype(jnp.float32) + update).astype(jnp.bfloat16)
        return carry

    lax.fori_loop(0, model // width, project, 0)
    normed_rows(first_v, normed_v)

    def swap(src_of, dst, slot):
        def step(shift, carry):
            other = lax.rem(tm + shift, TM)
            pltpu.make_async_remote_copy(
                src_ref=src_of(other),
                dst_ref=dst.at[tm],
                send_sem=swap_send.at[slot],
                recv_sem=swap_recv.at[slot],
                device_id=(clip, other),
                device_id_type=MESH,
            ).start()
            return carry

        lax.fori_loop(1, TM, step, 0)
        kept = pltpu.make_async_copy(src_of(tm), dst.at[tm], local_sem.at[8 + slot])
        kept.start()
        return kept

    def swapped(dst, kept, slot):
        ref = dst.at[pl.ds(0, TM - 1)]
        pltpu.make_async_copy(ref, ref, swap_recv.at[slot]).wait()
        kept.wait()

    def block_of(ref):
        return lambda index: ref.at[pl.ds(pl.multiple_of(index * per, per), per)]

    kept = swap(block_of(normed_v), spread_v, 0)

    temporal.first_near()
    for k in range(4):
        qkv.second_near(k)
    temporal.first_far()
    for k in range(4):
        qkv.second_far(k)

    rows = lax.broadcasted_iota(jnp.int32, (positions, TM), 0) // per
    cols16 = lax.broadcasted_iota(jnp.int32, (positions, TM), 1)
    frame_of = (rows == cols16).astype(jnp.float32)
    loads[7].wait()
    mask_f = jnp.where(mask_v[...] == 1, 1.0, 0.0)
    by_row = jnp.dot(frame_of, mask_f, preferred_element_type=jnp.float32)
    pairs = lax.dot_general(by_row, frame_of, (((1,), (1,)), ((), ())), preferred_element_type=jnp.float32)
    pos_r = lax.rem(lax.broadcasted_iota(jnp.int32, (positions, positions), 0), per)
    pos_c = lax.rem(lax.broadcasted_iota(jnp.int32, (positions, positions), 1), per)
    allowed_v[...] = jnp.where(pos_r == pos_c, pairs, 0.0)

    loads[5].wait()
    qkv.pushed()
    swapped(spread_v, kept, 0)

    def triple(chunk):
        cols = pl.ds(chunk * width, width)
        weights = qkv_w[:, :, cols].reshape(model, width)
        rows_in = spread_v[...].reshape(positions, model)
        qkv_v[:, cols] = jnp.dot(rows_in, weights, preferred_element_type=jnp.float32).astype(jnp.bfloat16)

    head_width = HEADS * HD
    for chunk in range(3 * head_width // width):
        triple(chunk)
        if chunk < 4:
            temporal.second_near(chunk)

    attend(
        qkv_v.at[:, pl.ds(0, head_width)],
        qkv_v.at[:, pl.ds(head_width, head_width)],
        qkv_v.at[:, pl.ds(2 * head_width, head_width)],
        wide_v, allowed_v, HEADS,
    )
    kept = swap(block_of(wide_v), home_v, 1)
    for k in range(4):
        temporal.second_far(k)
    loads[6].wait()
    temporal.pushed()
    swapped(home_v, kept, 1)

    def finish(chunk, carry):
        cols = pl.ds(pl.multiple_of(chunk * width, width), width)
        weights = proj_t[:, :, cols].reshape(head_width, width)
        rows_in = home_v[...].reshape(positions, head_width)
        update = jnp.dot(rows_in, weights, preferred_element_type=jnp.float32).astype(jnp.bfloat16)
        tok_v[:, cols] = (
            first_v[:, cols].astype(jnp.float32) + update.astype(jnp.float32)
        ).astype(jnp.bfloat16)
        return carry

    lax.fori_loop(0, model // width, finish, 0)
    put = pltpu.make_async_copy(tok_v, second_out, out_sem.at[0])
    put.start()
    ref = normed_v.at[pl.ds(0, positions - per)]
    pltpu.make_async_copy(ref, ref, swap_send.at[0]).wait()
    normed_rows(tok_v, normed_v)
    put2 = pltpu.make_async_copy(normed_v, routed_out, out_sem.at[1])
    put2.start()
    ref = wide_v.at[pl.ds(0, positions - per)]
    pltpu.make_async_copy(ref, ref, swap_send.at[1]).wait()
    spatial.drained()
    qkv.drained()
    temporal.drained()
    put.wait()
    put2.wait()


def trunk(tokens, sq, sk, sv, sproj, tqkv, tproj, mask):
    positions, model = tokens.shape
    head_width = sq.shape[1]
    per = positions // TM
    bf16 = jnp.bfloat16
    vm = lambda *shape: pltpu.VMEM(shape, bf16)
    any_spec = pl.BlockSpec(memory_space=pl.ANY)
    return pl.pallas_call(
        trunk_kernel,
        out_shape=(jax.ShapeDtypeStruct((positions, model), bf16),) * 2,
        in_specs=[any_spec] * 8,
        out_specs=(any_spec,) * 2,
        scratch_shapes=[
            vm(positions, model), vm(positions, head_width), vm(positions, head_width), vm(positions, head_width),
            vm(positions, head_width), vm(positions, model), vm(positions, model), vm(TM, per, model),
            vm(positions, 3 * head_width), vm(TM, per, head_width),
            pltpu.VMEM((positions, positions), jnp.float32), pltpu.VMEM((TM, TM), jnp.int32),
            vm(positions, head_width),
            vm(TM, sproj.shape[0], model), vm(TM, tqkv.shape[0], 3 * head_width), vm(TM, tproj.shape[0], model),
            pltpu.SemaphoreType.DMA((10,)), pltpu.SemaphoreType.DMA((3,)),
            pltpu.SemaphoreType.DMA((21,)), pltpu.SemaphoreType.DMA((21,)), pltpu.SemaphoreType.DMA((21,)),
            pltpu.SemaphoreType.DMA((2,)), pltpu.SemaphoreType.DMA((2,)), pltpu.SemaphoreType.DMA((2,)),
        ],
        compiler_params=pltpu.CompilerParams(
            collective_id=0, has_side_effects=True, vmem_limit_bytes=60 * 1024 * 1024
        ),
        name="trunk",
    )(tokens, sq, sk, sv, sproj, tqkv, tproj, mask)


def shards(
    tokens,
    spatial_queries,
    spatial_keys,
    spatial_values,
    spatial_proj,
    temporal_qkv,
    temporal_proj,
    frame_mask,
    expert_ids,
    gate_values,
    expert_gate,
    expert_up,
    expert_down,
):
    model_width = tokens.shape[3]
    positions = tokens.shape[2]
    tm_count = lax.axis_size("tm")
    clip_count = lax.axis_size("clip")
    experts = clip_count * tm_count
    second, routed = trunk(
        tokens.reshape(positions, model_width),
        spatial_queries.reshape(positions, -1),
        spatial_keys.reshape(positions, -1),
        spatial_values.reshape(positions, -1),
        spatial_proj,
        temporal_qkv,
        temporal_proj,
        frame_mask.reshape(frame_mask.shape[1:]),
    )
    capacity = 2 * TOP * positions // experts
    slot_count = experts * capacity
    pair_ids = expert_ids.reshape(positions * TOP)
    chosen = (pair_ids[:, None] == jnp.arange(experts, dtype=jnp.int32)[None, :]).astype(jnp.int32)
    earlier = jnp.cumsum(chosen, axis=0) - chosen
    pair_rank = jnp.sum(earlier * chosen, axis=1)
    pair_slot = pair_ids * capacity + pair_rank
    slot_index = jnp.arange(slot_count, dtype=jnp.int32)
    pair_onehot = (pair_slot[:, None] == slot_index[None, :]).astype(jnp.bfloat16)
    token_onehot = jnp.any(
        pair_slot.reshape(positions, TOP)[:, :, None] == slot_index[None, None, :], axis=1
    ).astype(jnp.bfloat16)
    outgoing = lax.dot_general(
        token_onehot, routed, (((0,), (0,)), ((), ())), preferred_element_type=jnp.float32
    )
    outgoing = outgoing.astype(jnp.bfloat16).reshape(experts, capacity, model_width)

    def expert_rows(received):
        flat_rows = received.reshape(-1, model_width)
        gate_part = jnp.dot(flat_rows, expert_gate[0], preferred_element_type=jnp.float32)
        up_part = jnp.dot(flat_rows, expert_up[0], preferred_element_type=jnp.float32)
        hidden = (jax.nn.silu(gate_part) * up_part).astype(jnp.bfloat16)
        answer = jnp.dot(hidden, expert_down[0], preferred_element_type=jnp.float32).astype(
            jnp.bfloat16
        )
        return answer.reshape(received.shape)

    def serve_slots(received):
        return lax.all_to_all(
            expert_rows(received), ("clip", "tm"), split_axis=0, concat_axis=0, tiled=True
        )

    answers = grouped_exchange(outgoing, ("clip", "tm"), 0, 0, serve_slots, 1, 1)
    pair_answers = jnp.dot(
        pair_onehot, answers.reshape(slot_count, model_width), preferred_element_type=jnp.float32
    )
    weighted = pair_answers.reshape(positions, TOP, model_width) * gate_values.reshape(
        positions, TOP, 1
    )
    expert_mix = jnp.sum(weighted, axis=1)
    layer_out = (second.astype(jnp.float32) + expert_mix).astype(jnp.bfloat16)
    return layer_out.reshape(tokens.shape)


def solution(mesh):
    placed = (
        P("clip", "tm", None, None),
        P("clip", "tm", None, None),
        P("clip", "tm", None, None),
        P("clip", "tm", None, None),
        P("tm", None),
        P("tm", None),
        P("tm", None),
        P("clip", None, None),
        P("clip", "tm", None, None),
        P("clip", "tm", None, None),
        P(("clip", "tm"), None, None),
        P(("clip", "tm"), None, None),
        P(("clip", "tm"), None, None),
    )
    return jax.shard_map(
        shards, mesh=mesh, in_specs=placed, out_specs=P("clip", "tm", None, None), check_vma=False
    )
```

time: 406 us -> 258 us (0.64)
  waiting for transfers between devices: 175 us -> 2.78 us
  Pallas kernels: 0 us -> 93.1 us
  matrix products: 72.7 us -> 51.2 us
  blocking collectives: 93.8 us -> 75.9 us
  between operations: 13.4 us -> 0.14 us
  starting transfers between devices: 26 us -> 15 us
    all_gather x3 -> x0, waiting for transfers between devices: 137 us -> none  [the longest x1 87.9 us: temporal_inputs(): lax.all_gather(qkv_rows, 'tm', axis=0, tiled=True)]
    pallas_call x0 -> x1, Pallas kernels: none -> 93.1 us  [trunk(): pl.pallas_call(trunk_kernel, out_shape=(jax.ShapeDtypeStruct((positions,...]
    all_to_all x3 -> x0, waiting for transfers between devices: 33.1 us -> none  [the longest x1 15.8 us: shards(): lax.all_to_all(blocks[:, :, 2 * head_width:], 'tm', split_axis=0, concat_...]
    dot_general x5 -> x0, matrix products: 19 us -> none  [the longest x3 15.6 us: add_columns(): return jnp.dot(left_side, piece, preferred_element_type=jnp.float32)]
    all_to_all x1 -> x0, blocking collectives: 17.8 us -> none  [shards(): lax.all_to_all(blocks[:, :, :head_width], 'tm', split_axis=0, concat_axis...]
    all_to_all x3 -> x0, starting transfers between devices: 10.9 us -> none  [the longest x1 3.75 us: shards(): lax.all_to_all(attended_time, 'tm', split_axis=0, concat_axis=0, tiled=True)]
  transfers between devices with their start and end apart: 8 -> 2, of which waited for: 6 -> 1; matrix products, arithmetic and copies ran while one was open for 20% -> 22% of each run, Pallas kernels for 0% -> 0%
where the time goes in v1:
time: 258 us
  Pallas kernels  93.1 us (36%)
  blocking collectives  75.9 us (29%)
  matrix products  51.2 us (20%)
  local copies, waits for them, and re-layouts  17.7 us (7%)
  starting transfers between devices  15 us (6%)
  waiting for transfers between devices  2.78 us (1%)
    pallas_call x1, Pallas kernels, trunk(): pl.pallas_call(trunk_kernel, out_shape=(jax.ShapeDtypeStruct((positions,...  93.1 us
    all_to_all x1, blocking collectives, moved(): lax.all_to_all(group, axis, split_axis=split_dim, concat_axis=concat_dim,...  39.4 us
    all_to_all x1, blocking collectives, serve_slots(): lax.all_to_all(expert_rows(received), ('clip', 'tm'), split_axis=0, conca...  36.5 us
    dot_general x2, matrix products, expert_rows(): jnp.dot(hidden, expert_down[0], preferred_element_type=jnp.float32)  27.2 us
    dot_general x2, matrix products, expert_rows(): jnp.dot(flat_rows, expert_gate[0], preferred_element_type=jnp.float32)  16.7 us
    all_to_all x1, starting transfers between devices, serve_slots(): lax.all_to_all(expert_rows(received), ('clip', 'tm'), split_axis=0, conca...  10.2 us
    reshape x2, local copies, waits for them, and re-layouts, expert_rows(): return answer.reshape(received.shape)  6.85 us
    reshape x2, local copies, waits for them, and re-layouts, expert_rows(): flat_rows = received.reshape(-1, model_width)  6.06 us
  transfers between devices with their start and end apart: 2, of which 1 were waited for; matrix products, arithmetic and copies ran while one was open for 22% of the time, Pallas kernels for 0%

profile of v1, /device:TPU:1, one launch (start us, length us, event | category | flops | bytes accessed | tf_op | source)
XLA Modules:
  0.0 258.0 jit_solution(14957810008623490533)
XLA Ops:
  0.0 0.8 copy.21
  0.8 0.1 eq.71
  1.0 0.1 eq.67
  1.1 0.1 copy.24
  1.2 0.2 fusion.44
  1.5 0.2 fusion.43
  1.8 0.1 reduce_sum.21
  1.9 0.1 copy.26
  2.0 0.3 fusion.35
  2.3 93.1 %trunk.1 = (bf16[256,2048]{1,0:T(8,128)(2,1)}, bf16[256,2048]{1,0:T(8,128)(2,1)}) custom-call(bf16[256,2048]{1,0:T(8,128)(2,1)} %bitcast.78, bf16[256,1024]{1,0:T(8,128)(2,1)} %bitcast.79, bf16[256,1024]{1,0:T(8,128)(2,1)} %bitcast.80, bf16[256,1024]{1,0:T(8,128)(2,1)} %bitcast.81, bf16[64,2048]{1,0:T(8,128)(2,1)} %sproj.1, bf16[128,3072]{1,0:T(8,128)(2,1)} %tqkv.1, ...), custom_call_target="tpu_custom_call" | custom-call | tf_op jit(solution)/shard_map/trunk/pallas_call | solution.py:366
  95.5 2.5 convert_bitcast_fusion
  98.0 3.3 %fusion.50 = (bf16[128,4,2048]{2,1,0:T(4,128)(2,1)}, bf16[128,4,2048]{2,1,0:T(4,128)(2,1)S(1)}) fusion(bf16[128,8,2048]{2,1,0:T(8,128)(2,1)S(1)} %convert_bitcast_fusion), kind=kLoop, calls=%fused_computation.45 | loop fusion | bytes 8388608 | tf_op jit(solution)/shard_map/slice | solution.py:31
  101.3 39.4 %all_to_all.20 = bf16[128,4,2048]{2,1,0:T(4,128)(2,1)} all-to-all(bf16[128,4,2048]{2,1,0:T(4,128)(2,1)S(1)} %get-tuple-element.10), channel_id=1, replica_groups=mesh['clip'=8,'tm'=16] {'clip','tm'}, dimensions={0} | all-to-all | bytes 4194304 | tf_op jit(solution)/shard_map/all_to_all | solution.py:26
  140.7 4.8 %all-to-all-start = ((bf16[128,4,2048]{2,1,0:T(4,128)(2,1)}), bf16[128,4,2048]{2,1,0:T(4,128)(2,1)S(1)}, u32[]{:S(2)}, u32[]{:S(2)}) async-start(bf16[128,4,2048]{2,1,0:T(4,128)(2,1)} %get-tuple-element.9), calls=%async_computation | async-start | bytes 4194304 | tf_op jit(solution)/shard_map/all_to_all | solution.py:26
  145.5 4.0 %reshape.110 = bf16[512,2048]{1,0:T(8,128)(2,1)} reshape(bf16[128,4,2048]{2,1,0:T(4,128)(2,1)} %all_to_all.20) | data formatting | bytes 4194304 | tf_op jit(solution)/shard_map/reshape | solution.py:437
  149.5 8.3 %fusion.8 = f32[512,1408]{1,0:T(8,128)} fusion(bf16[512,2048]{1,0:T(8,128)(2,1)} %reshape.110, bf16[1,2048,1408]{2,1,0:T(8,128)(2,1)} %param.23), kind=kOutput, calls=%fused_computation.8 | convolution fusion | flops 2952790016 | bytes 10747904 | tf_op jit(solution)/shard_map/dot_general | solution.py:438
  157.7 13.9 %fusion.30 = bf16[512,2048]{1,0:T(8,128)(2,1)} fusion(bf16[1,1408,2048]{2,1,0:T(8,128)(2,1)} %param.25, bf16[512,2048]{1,0:T(8,128)(2,1)} %reshape.110, bf16[1,2048,1408]{2,1,0:T(8,128)(2,1)} %param.24, f32[512,1408]{1,0:T(8,128)} %fusion.8), kind=kOutput, calls=%fused_computation.23 | convolution fusion | flops 5910953984 | bytes 18612224 | tf_op jit(solution)/shard_map/dot_general | solution.py:441
  171.6 4.1 %reshape.111 = bf16[128,4,2048]{2,1,0:T(4,128)(2,1)} reshape(bf16[512,2048]{1,0:T(8,128)(2,1)} %fusion.30) | data formatting | bytes 4194304 | tf_op jit(solution)/shard_map/reshape | solution.py:444
  175.7 0.0 all-to-all-done
  175.7 10.2 %all-to-all-start.3 = ((bf16[128,4,2048]{2,1,0:T(4,128)(2,1)}), bf16[128,4,2048]{2,1,0:T(4,128)(2,1)}, u32[]{:S(2)}, u32[]{:S(2)}) async-start(bf16[128,4,2048]{2,1,0:T(4,128)(2,1)} %reshape.111), calls=%async_computation.3 | async-start | bytes 4194304 | tf_op jit(solution)/shard_map/all_to_all | solution.py:447
  186.0 2.1 reshape.108
  188.1 8.4 %fusion.10 = f32[512,1408]{1,0:T(8,128)} fusion(bf16[512,2048]{1,0:T(8,128)(2,1)} %reshape.108, bf16[1,2048,1408]{2,1,0:T(8,128)(2,1)} %param.23), kind=kOutput, calls=%fused_computation.10 | convolution fusion | flops 2952790016 | bytes 10747904 | tf_op jit(solution)/shard_map/dot_general | solution.py:438
  196.5 0.0 copy-done
  196.5 13.3 %fusion.27 = bf16[512,2048]{1,0:T(8,128)(2,1)} fusion(bf16[1,1408,2048]{2,1,0:T(8,128)(2,1)} %param.25, bf16[512,2048]{1,0:T(8,128)(2,1)S(1)} %copy-done, bf16[1,2048,1408]{2,1,0:T(8,128)(2,1)} %param.24, f32[512,1408]{1,0:T(8,128)} %fusion.10), kind=kOutput, calls=%fused_computation.22 | convolution fusion | flops 5910953984 | bytes 18612224 | tf_op jit(solution)/shard_map/dot_general | solution.py:441
  209.8 2.7 %reshape.109 = bf16[128,4,2048]{2,1,0:T(4,128)(2,1)S(1)} reshape(bf16[512,2048]{1,0:T(8,128)(2,1)} %fusion.27) | data formatting | bytes 4194304 | tf_op jit(solution)/shard_map/reshape | solution.py:444
  212.5 0.0 copy-start.2
  212.5 2.8 %all-to-all-done.3 = bf16[128,4,2048]{2,1,0:T(4,128)(2,1)} async-done(((bf16[128,4,2048]{2,1,0:T(4,128)(2,1)}), bf16[128,4,2048]{2,1,0:T(4,128)(2,1)}, u32[]{:S(2)}, u32[]{:S(2)}) %all-to-all-start.3) | async-done | bytes 2097184 | tf_op jit(solution)/shard_map/all_to_all | solution.py:447
  215.3 36.5 %all_to_all.21 = bf16[128,4,2048]{2,1,0:T(4,128)(2,1)S(1)} all-to-all(bf16[128,4,2048]{2,1,0:T(4,128)(2,1)S(1)} %reshape.109), channel_id=1, replica_groups=mesh['clip'=8,'tm'=16] {'clip','tm'}, dimensions={0} | all-to-all | bytes 4194304 | tf_op jit(solution)/shard_map/all_to_all | solution.py:447
  251.8 0.0 copy-done.2
  251.8 4.9 %multiply_reduce_fusion = f32[256,2048]{1,0:T(8,128)S(1)} fusion(bf16[128,4,2048]{2,1,0:T(4,128)(2,1)} %all-to-all-done.3, bf16[128,4,2048]{2,1,0:T(4,128)(2,1)S(1)} %all_to_all.21, f32[256,2]{0,1:T(2,128)S(1)} %bitcast.84, s32[256,2]{0,1:T(2,128)S(1)} %copy.26), kind=kOutput, calls=%fused_computation.16 | convolution fusion | flops 2157969408 | bytes 6295552 | tf_op jit(solution)/shard_map/dot_general | solution.py:452
  256.7 0.0 copy-done.1
  256.7 1.3 fusion.36
  (9 shorter events, 0.1 us)
Async XLA Ops:
  140.7 35.0 %all-to-all-start = ((bf16[128,4,2048]{2,1,0:T(4,128)(2,1)}), bf16[128,4,2048]{2,1,0:T(4,128)(2,1)S(1)}, u32[]{:S(2)}, u32[]{:S(2)}) async-start(bf16[128,4,2048]{2,1,0:T(4,128)(2,1)} %get-tuple-element.9), calls=%async_computation | async-start | bytes 4194304 | tf_op jit(solution)/shard_map/all_to_all | solution.py:26
  175.7 39.6 %all-to-all-start.3 = ((bf16[128,4,2048]{2,1,0:T(4,128)(2,1)}), bf16[128,4,2048]{2,1,0:T(4,128)(2,1)}, u32[]{:S(2)}, u32[]{:S(2)}) async-start(bf16[128,4,2048]{2,1,0:T(4,128)(2,1)} %reshape.111), calls=%async_computation.3 | async-start | bytes 4194304 | tf_op jit(solution)/shard_map/all_to_all | solution.py:447
  188.1 8.4 %copy-start = (bf16[512,2048]{1,0:T(8,128)(2,1)S(1)}, bf16[512,2048]{1,0:T(8,128)(2,1)}, u32[]{:S(2)}) copy-start(bf16[512,2048]{1,0:T(8,128)(2,1)} %reshape.108) | copy-start | bytes 6291460
  212.5 39.3 %copy-start.2 = (f32[1,1,256,2]{2,3,1,0:T(2,128)S(1)}, f32[1,1,256,2]{2,3,1,0:T(2,128)}, u32[]{:S(2)}) copy-start(f32[1,1,256,2]{2,3,1,0:T(2,128)} %param.22) | copy-start | bytes 6148
  251.8 4.9 %copy-start.1 = (bf16[256,2048]{1,0:T(8,128)(2,1)S(1)}, bf16[256,2048]{1,0:T(8,128)(2,1)}, u32[]{:S(2)}) copy-start(bf16[256,2048]{1,0:T(8,128)(2,1)} %get-tuple-element.7) | copy-start | bytes 3145732

commit v2 on v1

--- a/solution.py
+++ b/solution.py
@@ -1,4 +1,3 @@
-import functools
 import math
 
 import jax
@@ -11,6 +10,7 @@
 HEADS = 8
 HD = 128
 TOP = 2
+CAP = 8
 SIDE = 4
 TM = 16
 
@@ -18,22 +18,10 @@
 EPS = 1e-06
 MASKED = -1e30
 MESH = pl.DeviceIdType.MESH
-
-
-def grouped_exchange(x, axis, split_dim, concat_dim, work, item_dim, out_dim):
-
-    def moved(group):
-        return lax.all_to_all(group, axis, split_axis=split_dim, concat_axis=concat_dim, tiled=True)
-
-    items = jax.tree.leaves(x)[0].shape[item_dim]
-    ends = [items * k // 2 for k in range(2 + 1)] if items % 2 == 0 else [0, items]
-    groups = [
-        jax.tree.map(lambda a: lax.slice_in_dim(a, low, high, axis=item_dim), x)
-        for low, high in zip(ends, ends[1:])
-    ]
-    arrived = [moved(group) for group in groups]
-    made = [work(group) for group in arrived]
-    return jax.tree.map(lambda *parts: jnp.concatenate(parts, axis=out_dim), *made)
+STRIDE = 49
+INVERSE = pow(STRIDE, -1, 128)
+GROUPS = 4
+DEVICES = 128
 
 
 class Gather:
@@ -170,12 +158,13 @@
     lax.fori_loop(0, heads // 2, step, 0)
 
 
-def trunk_kernel(
-    tokens, sq, sk, sv, sproj, tqkv, tproj, mask,
-    second_out, routed_out,
-    tok_v, q_v, k_v, v_v, mixed_v, first_v, normed_v, spread_v, qkv_v, home_v, allowed_v, mask_v,
-    wide_v, proj_s, qkv_w, proj_t,
-    local_sem, send_sem, recv_s, recv_q, recv_t, swap_send, swap_recv, out_sem,
+def layer_kernel(
+    tokens, sq, sk, sv, sproj, tqkv, tproj, mask, ids, gates, w_gate, w_up, w_down,
+    out,
+    tok_v, mixed_v, normed_v, spread_v, qkv_v, home_v, allowed_v, mask_v, ids_v, gates_v,
+    proj_s, qkv_w, proj_t, gate_w, up_w, down_w, outgoing, received, answers, hidden_v, total_v,
+    slots_v, slots_t,
+    local_sem, send_sem, recv_s, recv_q, recv_t, swap_send, swap_recv, moe_send, go_recv, back_recv,
 ):
     clip = lax.axis_index("clip")
     tm = lax.axis_index("tm")
@@ -183,6 +172,8 @@
     y, x = tm // SIDE, lax.rem(tm, SIDE)
     positions = tok_v.shape[0]
     per = positions // TM
+    head_width = HEADS * HD
+    me = clip * TM + tm
     place = {
         "clip": clip,
         "tm": tm,
@@ -201,32 +192,39 @@
         pltpu.make_async_copy(src, dst, local_sem.at[n])
         for n, (src, dst) in enumerate(
             [
-                (sq, q_v), (sk, k_v), (sv, v_v), (tokens, tok_v),
+                (sq, qkv_v.at[:, pl.ds(0, head_width)]),
+                (sk, qkv_v.at[:, pl.ds(head_width, head_width)]),
+                (sv, qkv_v.at[:, pl.ds(2 * head_width, head_width)]),
+                (tokens, tok_v),
                 (sproj, proj_s.at[tm]), (tqkv, qkv_w.at[tm]), (tproj, proj_t.at[tm]), (mask, mask_v),
+                (ids, ids_v), (gates, gates_v), (w_gate, gate_w), (w_up, up_w), (w_down, down_w),
             ]
         )
     ]
-    for load in loads:
+    for load in loads[:10]:
         load.start()
 
     barrier = pltpu.get_barrier_semaphore()
 
     def greet(step, carry):
+        other = lax.rem(me + step, DEVICES)
         pl.semaphore_signal(
-            barrier, inc=1, device_id=(clip, lax.rem(tm + step, TM)), device_id_type=MESH
+            barrier, inc=1, device_id=(other // TM, lax.rem(other, TM)), device_id_type=MESH
         )
         return carry
 
-    lax.fori_loop(1, TM, greet, 0)
-    pl.semaphore_signal(barrier, inc=1, device_id=(place["partner"], tm), device_id_type=MESH)
-    pl.semaphore_wait(barrier, TM)
+    lax.fori_loop(1, DEVICES, greet, 0)
+    pl.semaphore_wait(barrier, DEVICES - 1)
 
     spatial.own()
     qkv.own()
 
     for n in (0, 1, 2):
         loads[n].wait()
-    attend(q_v, k_v, v_v, mixed_v, None, HEADS)
+    triple_of = [qkv_v.at[:, pl.ds(n * head_width, head_width)] for n in range(3)]
+    attend(*triple_of, mixed_v, None, HEADS)
+    for load in loads[10:]:
+        load.start()
 
     spatial.first_near()
     spatial.first_far()
@@ -248,11 +246,11 @@
         cols = pl.ds(pl.multiple_of(chunk * width, width), width)
         weights = proj_s[:, :, cols].reshape(mixed_v.shape[1], width)
         update = jnp.dot(mixed_v[...], weights, preferred_element_type=jnp.float32)
-        first_v[:, cols] = (tok_v[:, cols].astype(jnp.float32) + update).astype(jnp.bfloat16)
+        tok_v[:, cols] = (tok_v[:, cols].astype(jnp.float32) + update).astype(jnp.bfloat16)
         return carry
 
     lax.fori_loop(0, model // width, project, 0)
-    normed_rows(first_v, normed_v)
+    normed_rows(tok_v, normed_v)
 
     def swap(src_of, dst, slot):
         def step(shift, carry):
@@ -268,7 +266,7 @@
             return carry
 
         lax.fori_loop(1, TM, step, 0)
-        kept = pltpu.make_async_copy(src_of(tm), dst.at[tm], local_sem.at[8 + slot])
+        kept = pltpu.make_async_copy(src_of(tm), dst.at[tm], local_sem.at[13 + slot])
         kept.start()
         return kept
 
@@ -300,6 +298,8 @@
     pos_c = lax.rem(lax.broadcasted_iota(jnp.int32, (positions, positions), 1), per)
     allowed_v[...] = jnp.where(pos_r == pos_c, pairs, 0.0)
 
+    number_slots(ids_v, slots_v, slots_t, loads[8], clip, tm)
+
     loads[5].wait()
     qkv.pushed()
     swapped(spread_v, kept, 0)
@@ -310,19 +310,13 @@
         rows_in = spread_v[...].reshape(positions, model)
         qkv_v[:, cols] = jnp.dot(rows_in, weights, preferred_element_type=jnp.float32).astype(jnp.bfloat16)
 
-    head_width = HEADS * HD
     for chunk in range(3 * head_width // width):
         triple(chunk)
         if chunk < 4:
             temporal.second_near(chunk)
 
-    attend(
-        qkv_v.at[:, pl.ds(0, head_width)],
-        qkv_v.at[:, pl.ds(head_width, head_width)],
-        qkv_v.at[:, pl.ds(2 * head_width, head_width)],
-        wide_v, allowed_v, HEADS,
-    )
-    kept = swap(block_of(wide_v), home_v, 1)
+    attend(*triple_of, mixed_v, allowed_v, HEADS)
+    kept = swap(block_of(mixed_v), home_v, 1)
     for k in range(4):
         temporal.second_far(k)
     loads[6].wait()
@@ -335,55 +329,213 @@
         rows_in = home_v[...].reshape(positions, head_width)
         update = jnp.dot(rows_in, weights, preferred_element_type=jnp.float32).astype(jnp.bfloat16)
         tok_v[:, cols] = (
-            first_v[:, cols].astype(jnp.float32) + update.astype(jnp.float32)
+            tok_v[:, cols].astype(jnp.float32) + update.astype(jnp.float32)
         ).astype(jnp.bfloat16)
         return carry
 
     lax.fori_loop(0, model // width, finish, 0)
-    put = pltpu.make_async_copy(tok_v, second_out, out_sem.at[0])
-    put.start()
     ref = normed_v.at[pl.ds(0, positions - per)]
     pltpu.make_async_copy(ref, ref, swap_send.at[0]).wait()
     normed_rows(tok_v, normed_v)
-    put2 = pltpu.make_async_copy(normed_v, routed_out, out_sem.at[1])
-    put2.start()
-    ref = wide_v.at[pl.ds(0, positions - per)]
+
+    size = DEVICES // GROUPS
+    slots = size * CAP
+
+    def peer(order, sign):
+        offset = lax.rem(order * STRIDE, DEVICES)
+        dz, dc = lax.rem(offset, 4), lax.rem(offset // 4, 2)
+        dy, dx = lax.rem(offset // 8, 4), offset // 32
+        to_z = lax.rem(clip // 2 + sign * dz + 4, 4)
+        to_c = lax.rem(core + dc, 2)
+        to_y = lax.rem(y + sign * dy + 4, 4)
+        to_x = lax.rem(x + sign * dx + 4, 4)
+        return to_z * 2 + to_c, to_y * 4 + to_x
+
+    def ship(group, sign, src, dst, sends, receives):
+        def step(order, carry):
+            to_clip, to_tm = peer(order, sign)
+
+            @pl.when(order > 0)
+            def _():
+                pltpu.make_async_remote_copy(
+                    src_ref=src.at[order],
+                    dst_ref=dst.at[order],
+                    send_sem=sends,
+                    recv_sem=receives.at[group],
+                    device_id=(to_clip, to_tm),
+                    device_id_type=MESH,
+                ).start()
+
+            return carry
+
+        lax.fori_loop(group * size, group * size + size, step, 0)
+
+    def landed(group, dst, receives):
+        ref = dst.at[pl.ds(0, size)]
+        pltpu.make_async_copy(ref, ref, receives.at[group]).wait()
+
+    def pick(group, table):
+        return (lax.broadcasted_iota(jnp.int32, (slots, positions), 0) + group * slots == table).astype(
+            jnp.float32
+        )
+
+    def build(group, carry):
+        chosen = pick(group, slots_t[0:1, :]) + pick(group, slots_t[1:2, :])
+        chosen = chosen.astype(jnp.bfloat16)
+        for chunk in range(model // width):
+            cols = pl.ds(chunk * width, width)
+            rows_out = jnp.dot(chosen, normed_v[:, cols], preferred_element_type=jnp.float32)
+            outgoing[pl.ds(group * size, size), :, cols] = rows_out.reshape(size, CAP, width).astype(
+                jnp.bfloat16
+            )
+        ship(group, 1, outgoing, received, moe_send.at[0], go_recv)
+        return carry
+
+    lax.fori_loop(0, GROUPS, build, 0)
+    pltpu.make_async_copy(outgoing.at[0], received.at[0], go_recv.at[0]).start()
+    for load in loads[9:]:
+        load.wait()
+
+    def serve(group, carry):
+        landed(group, received, go_recv)
+        mine = pl.ds(group * size, size)
+        for chunk in range(model // width):
+            cols = pl.ds(chunk * width, width)
+            wide = received[mine, :, cols].astype(jnp.float32)
+            normed_v[:, cols] = wide.reshape(slots, width).astype(jnp.bfloat16)
+
+        def gate_up(cols):
+            rows_in = normed_v[...]
+            gate_part = jnp.dot(rows_in, gate_w[:, cols], preferred_element_type=jnp.float32)
+            up_part = jnp.dot(rows_in, up_w[:, cols], preferred_element_type=jnp.float32)
+            hidden_v[:, cols] = (gate_part / (1.0 + jnp.exp(-gate_part)) * up_part).astype(jnp.bfloat16)
+
+        def gate_step(chunk, carry):
+            gate_up(pl.ds(pl.multiple_of(chunk * 256, 256), 256))
+            return carry
+
+        hidden = hidden_v.shape[1]
+        lax.fori_loop(0, hidden // 256, gate_step, 0)
+        if hidden % 256:
+            gate_up(pl.ds(hidden - hidden % 256, hidden % 256))
+
+        def down_step(chunk, carry):
+            cols = pl.ds(pl.multiple_of(chunk * width, width), width)
+            answer = jnp.dot(hidden_v[...], down_w[:, cols], preferred_element_type=jnp.float32)
+            received[mine, :, cols] = answer.reshape(size, CAP, width).astype(jnp.bfloat16)
+            return carry
+
+        lax.fori_loop(0, model // width, down_step, 0)
+        ship(group, -1, received, answers, moe_send.at[1], back_recv)
+
+        @pl.when(group == 0)
+        def _():
+            pltpu.make_async_copy(received.at[0], answers.at[0], back_recv.at[0]).start()
+
+        return carry
+
+    lax.fori_loop(0, GROUPS, serve, 0)
+
+    def combine(group, carry):
+        landed(group, answers, back_recv)
+        lanes = lax.broadcasted_iota(jnp.int32, (positions, slots), 1) + group * slots
+        picks = [
+            (lanes == slots_v[:, k : k + 1]).astype(jnp.float32).astype(jnp.bfloat16) for k in range(TOP)
+        ]
+        for chunk in range(model // width):
+            cols = pl.ds(chunk * width, width)
+            wide = answers[pl.ds(group * size, size), :, cols].astype(jnp.float32)
+            rows_in = wide.reshape(slots, width).astype(jnp.bfloat16)
+            parts = [
+                jnp.dot(picks[k], rows_in, preferred_element_type=jnp.float32) * gates_v[:, k : k + 1]
+                for k in range(TOP)
+            ]
+            part = parts[0] + parts[1]
+
+            @pl.when(group == 0)
+            def _():
+                total_v[:, cols] = part
+
+            @pl.when(group > 0)
+            def _():
+                total_v[:, cols] = total_v[:, cols] + part
+
+        return carry
+
+    lax.fori_loop(0, GROUPS, combine, 0)
+
+    def close(block, carry):
+        rows_at = pl.ds(pl.multiple_of(block * 32, 32), 32)
+        tok_v[rows_at, :] = (tok_v[rows_at, :].astype(jnp.float32) + total_v[rows_at, :]).astype(jnp.bfloat16)
+        return carry
+
+    lax.fori_loop(0, positions // 32, close, 0)
+    put = pltpu.make_async_copy(tok_v, out, local_sem.at[15])
+    put.start()
+    ref = mixed_v.at[pl.ds(0, positions - per)]
     pltpu.make_async_copy(ref, ref, swap_send.at[1]).wait()
     spatial.drained()
     qkv.drained()
     temporal.drained()
+    ref = outgoing.at[pl.ds(0, DEVICES - 1)]
+    pltpu.make_async_copy(ref, ref, moe_send.at[0]).wait()
+    pltpu.make_async_copy(ref, ref, moe_send.at[1]).wait()
     put.wait()
-    put2.wait()
-
-
-def trunk(tokens, sq, sk, sv, sproj, tqkv, tproj, mask):
+
+
+def number_slots(ids_v, slots_v, slots_t, load, clip, tm):
+    load.wait()
+    positions = ids_v.shape[0]
+    expert = lax.broadcasted_iota(jnp.int32, (positions, DEVICES), 1)
+    e_clip, e_tm = expert // TM, lax.rem(expert, TM)
+    dz = lax.rem(e_clip // 2 - clip // 2 + 4, 4)
+    dc = lax.rem(lax.rem(e_clip, 2) - lax.rem(clip, 2) + 2, 2)
+    dy = lax.rem(e_tm // SIDE - tm // SIDE + 4, 4)
+    dx = lax.rem(lax.rem(e_tm, SIDE) - lax.rem(tm, SIDE) + 4, 4)
+    order = lax.rem((dz + 4 * dc + 8 * dy + 32 * dx) * INVERSE, DEVICES)
+    named = [(ids_v[:, k : k + 1] == expert).astype(jnp.float32) for k in range(TOP)]
+    rows = lax.broadcasted_iota(jnp.int32, (positions, positions), 0)
+    cols = lax.broadcasted_iota(jnp.int32, (positions, positions), 1)
+    before = (cols < rows).astype(jnp.float32).astype(jnp.bfloat16)
+    counts = jnp.dot(before, (named[0] + named[1]).astype(jnp.bfloat16), preferred_element_type=jnp.float32)
+    row = (order * CAP).astype(jnp.float32) + counts
+    found = [jnp.sum(named[k] * row, axis=1, keepdims=True) for k in range(TOP)]
+    table = jnp.where(expert == 0, found[0], jnp.where(expert == 1, found[1], -1.0))
+    slots_v[...] = table.astype(jnp.int32)
+    slots_t[...] = table.T.astype(jnp.int32)
+
+
+def layer(tokens, sq, sk, sv, sproj, tqkv, tproj, mask, ids, gates, w_gate, w_up, w_down):
     positions, model = tokens.shape
     head_width = sq.shape[1]
     per = positions // TM
+    hidden = w_gate.shape[1]
     bf16 = jnp.bfloat16
     vm = lambda *shape: pltpu.VMEM(shape, bf16)
+    dma = lambda n: pltpu.SemaphoreType.DMA((n,))
     any_spec = pl.BlockSpec(memory_space=pl.ANY)
     return pl.pallas_call(
-        trunk_kernel,
-        out_shape=(jax.ShapeDtypeStruct((positions, model), bf16),) * 2,
-        in_specs=[any_spec] * 8,
-        out_specs=(any_spec,) * 2,
+        layer_kernel,
+        out_shape=jax.ShapeDtypeStruct((positions, model), bf16),
+        in_specs=[any_spec] * 13,
+        out_specs=any_spec,
         scratch_shapes=[
-            vm(positions, model), vm(positions, head_width), vm(positions, head_width), vm(positions, head_width),
-            vm(positions, head_width), vm(positions, model), vm(positions, model), vm(TM, per, model),
+            vm(positions, model), vm(positions, head_width), vm(positions, model), vm(TM, per, model),
             vm(positions, 3 * head_width), vm(TM, per, head_width),
             pltpu.VMEM((positions, positions), jnp.float32), pltpu.VMEM((TM, TM), jnp.int32),
-            vm(positions, head_width),
+            pltpu.VMEM((positions, TOP), jnp.int32), pltpu.VMEM((positions, TOP), jnp.float32),
             vm(TM, sproj.shape[0], model), vm(TM, tqkv.shape[0], 3 * head_width), vm(TM, tproj.shape[0], model),
-            pltpu.SemaphoreType.DMA((10,)), pltpu.SemaphoreType.DMA((3,)),
-            pltpu.SemaphoreType.DMA((21,)), pltpu.SemaphoreType.DMA((21,)), pltpu.SemaphoreType.DMA((21,)),
-            pltpu.SemaphoreType.DMA((2,)), pltpu.SemaphoreType.DMA((2,)), pltpu.SemaphoreType.DMA((2,)),
+            vm(model, hidden), vm(model, hidden), vm(hidden, model),
+            vm(DEVICES, CAP, model), vm(DEVICES, CAP, model), vm(DEVICES, CAP, model),
+            vm(positions, hidden), pltpu.VMEM((positions, model), jnp.float32),
+            pltpu.VMEM((positions, DEVICES), jnp.int32), pltpu.VMEM((DEVICES, positions), jnp.int32),
+            dma(16), dma(3), dma(21), dma(21), dma(21), dma(2), dma(2), dma(2), dma(GROUPS), dma(GROUPS),
         ],
         compiler_params=pltpu.CompilerParams(
-            collective_id=0, has_side_effects=True, vmem_limit_bytes=60 * 1024 * 1024
+            collective_id=0, has_side_effects=True, vmem_limit_bytes=67043328
         ),
-        name="trunk",
-    )(tokens, sq, sk, sv, sproj, tqkv, tproj, mask)
+        name="layer",
+    )(tokens, sq, sk, sv, sproj, tqkv, tproj, mask, ids, gates, w_gate, w_up, w_down)
 
 
 def shards(
@@ -401,12 +553,8 @@
     expert_up,
     expert_down,
 ):
-    model_width = tokens.shape[3]
-    positions = tokens.shape[2]
-    tm_count = lax.axis_size("tm")
-    clip_count = lax.axis_size("clip")
-    experts = clip_count * tm_count
-    second, routed = trunk(
+    positions, model_width = tokens.shape[2:]
+    layer_out = layer(
         tokens.reshape(positions, model_width),
         spatial_queries.reshape(positions, -1),
         spatial_keys.reshape(positions, -1),
@@ -415,48 +563,12 @@
         temporal_qkv,
         temporal_proj,
         frame_mask.reshape(frame_mask.shape[1:]),
+        expert_ids.reshape(positions, TOP),
+        gate_values.reshape(positions, TOP),
+        expert_gate[0],
+        expert_up[0],
+        expert_down[0],
     )
-    capacity = 2 * TOP * positions // experts
-    slot_count = experts * capacity
-    pair_ids = expert_ids.reshape(positions * TOP)
-    chosen = (pair_ids[:, None] == jnp.arange(experts, dtype=jnp.int32)[None, :]).astype(jnp.int32)
-    earlier = jnp.cumsum(chosen, axis=0) - chosen
-    pair_rank = jnp.sum(earlier * chosen, axis=1)
-    pair_slot = pair_ids * capacity + pair_rank
-    slot_index = jnp.arange(slot_count, dtype=jnp.int32)
-    pair_onehot = (pair_slot[:, None] == slot_index[None, :]).astype(jnp.bfloat16)
-    token_onehot = jnp.any(
-        pair_slot.reshape(positions, TOP)[:, :, None] == slot_index[None, None, :], axis=1
-    ).astype(jnp.bfloat16)
-    outgoing = lax.dot_general(
-        token_onehot, routed, (((0,), (0,)), ((), ())), preferred_element_type=jnp.float32
-    )
-    outgoing = outgoing.astype(jnp.bfloat16).reshape(experts, capacity, model_width)
-
-    def expert_rows(received):
-        flat_rows = received.reshape(-1, model_width)
-        gate_part = jnp.dot(flat_rows, expert_gate[0], preferred_element_type=jnp.float32)
-        up_part = jnp.dot(flat_rows, expert_up[0], preferred_element_type=jnp.float32)
-        hidden = (jax.nn.silu(gate_part) * up_part).astype(jnp.bfloat16)
-        answer = jnp.dot(hidden, expert_down[0], preferred_element_type=jnp.float32).astype(
-            jnp.bfloat16
-        )
-        return answer.reshape(received.shape)
-
-    def serve_slots(received):
-        return lax.all_to_all(
-            expert_rows(received), ("clip", "tm"), split_axis=0, concat_axis=0, tiled=True
-        )
-
-    answers = grouped_exchange(outgoing, ("clip", "tm"), 0, 0, serve_slots, 1, 1)
-    pair_answers = jnp.dot(
-        pair_onehot, answers.reshape(slot_count, model_width), preferred_element_type=jnp.float32
-    )
-    weighted = pair_answers.reshape(positions, TOP, model_width) * gate_values.reshape(
-        positions, TOP, 1
-    )
-    expert_mix = jnp.sum(weighted, axis=1)
-    layer_out = (second.astype(jnp.float32) + expert_mix).astype(jnp.bfloat16)
     return layer_out.reshape(tokens.shape)
 
 

time: 258 us -> 202 us (0.78)
  Pallas kernels: 93.1 us -> 197 us
  blocking collectives: 75.9 us -> 0 us
  matrix products: 51.2 us -> 0 us
  starting transfers between devices: 15 us -> 0 us
  local copies, waits for them, and re-layouts: 17.7 us -> 5.24 us
  waiting for transfers between devices: 2.78 us -> 0 us
    pallas_call x1, Pallas kernels: 93.1 us -> 197 us  [layer(): pl.pallas_call(layer_kernel, out_shape=jax.ShapeDtypeStruct((positions, m...]
    all_to_all x2 -> x0, blocking collectives: 75.9 us -> none  [the longest x1 39.4 us: moved(): lax.all_to_all(group, axis, split_axis=split_dim, concat_axis=concat_dim,...]
    dot_general x6 -> x0, matrix products: 51.2 us -> none  [the longest x2 27.2 us: expert_rows(): jnp.dot(hidden, expert_down[0], preferred_element_type=jnp.float32)]
    all_to_all x2 -> x0, starting transfers between devices: 15 us -> none  [the longest x1 10.2 us: serve_slots(): lax.all_to_all(expert_rows(received), ('clip', 'tm'), split_axis=0, conca...]
    reshape x4 -> x0, local copies, waits for them, and re-layouts: 12.9 us -> none  [the longest x2 6.85 us: expert_rows(): return answer.reshape(received.shape)]
    unnamed x8 -> x3, local copies, waits for them, and re-layouts: 0.83 us -> 5.24 us
    slice x1 -> x0, local copies, waits for them, and re-layouts: 3.32 us -> none  [grouped_exchange(): lax.slice_in_dim(a, low, high, axis=item_dim)]
    all_to_all x2 -> x0, waiting for transfers between devices: 2.78 us -> none  [the longest x1 2.78 us: serve_slots(): lax.all_to_all(expert_rows(received), ('clip', 'tm'), split_axis=0, conca...]
  transfers between devices with their start and end apart: 2 -> 0, of which waited for: 1 -> 0; matrix products, arithmetic and copies ran while one was open for 22% -> 0% of each run, Pallas kernels for 0% -> 0%
where the time goes in v2:
time: 202 us
  Pallas kernels  197 us (98%)
  local copies, waits for them, and re-layouts  5.24 us (3%)
    pallas_call x1, Pallas kernels, layer(): pl.pallas_call(layer_kernel, out_shape=jax.ShapeDtypeStruct((positions, m...  197 us
    unnamed x3, local copies, waits for them, and re-layouts  5.24 us

profile of v2, /device:TPU:1, one launch (start us, length us, event | category | flops | bytes accessed | tf_op | source)
XLA Modules:
  0.0 202.2 jit_solution(14524338633238358768)
XLA Ops:
  0.0 1.5 copy.14
  1.5 1.5 copy.15
  2.9 196.9 %layer.1 = bf16[256,2048]{1,0:T(8,128)(2,1)} custom-call(bf16[256,2048]{1,0:T(8,128)(2,1)} %bitcast.15, bf16[256,1024]{1,0:T(8,128)(2,1)} %bitcast.18, bf16[256,1024]{1,0:T(8,128)(2,1)} %bitcast.19, bf16[256,1024]{1,0:T(8,128)(2,1)} %bitcast.20, bf16[64,2048]{1,0:T(8,128)(2,1)} %sproj.1, bf16[128,3072]{1,0:T(8,128)(2,1)} %tqkv.1, bf16[64,2048]{1,0:T(8,128)(2,1)} %tproj.1, ...), custom_call_target="tpu_custom_call" | custom-call | tf_op jit(solution)/shard_map/layer/pallas_call | solution.py:517
  199.9 2.3 %copy.17 = bf16[1,1,256,2048]{3,2,1,0:T(8,128)(2,1)} copy(bf16[1,1,256,2048]{3,2,1,0:T(8,128)(2,1)} %bitcast.14) | data formatting | bytes 2097152

commit v3 on v2

--- a/solution.py
+++ b/solution.py
@@ -25,24 +25,33 @@
 
 
 class Gather:
-    def __init__(self, shard, full, place, send, recv):
+    OFFSETS = (0, -1, 1, 2)
+    EVENTS = ((-1, 0), (1, 0), (2, 0)) + tuple((i, j) for i in (0, -1, 1, 2) for j in (-1, 1)) + tuple(
+        (i, 2) for i in (0, -1, 1, 2)
+    )
+
+    def __init__(self, shard, full, start, columns, place, send, recv, split):
         self.shard, self.full, self.send, self.recv = shard, full, send, recv
+        self.start, self.columns, self.place, self.split = start, columns, place, split
         self.rows = full.shape[1]
-        self.place = place
-
-    def part(self, index, quarter=None):
-        half = self.rows // 2
-        if quarter is None:
-            start = pl.multiple_of(self.place["core"] * half, half)
-            return self.full.at[index, pl.ds(start, half)]
-        size = half // 2
-        start = pl.multiple_of(self.place["core"] * half + quarter * size, size)
-        return self.full.at[index, pl.ds(start, size)]
+        self.size = self.rows // 4 if split else self.rows // 2
+        if split:
+            self.base = place["parity"] * (self.rows // 2) + place["core"] * self.size
+            self.other = (1 - place["parity"]) * (self.rows // 2) + place["core"] * self.size
+        else:
+            self.base = place["core"] * self.size
+
+    def span(self, part):
+        if part is None:
+            return pl.ds(self.start, self.columns)
+        return pl.ds(self.start + part * (self.columns // 2), self.columns // 2)
+
+    def part(self, index, part=None, base=None):
+        base = self.base if base is None else base
+        return self.full.at[index, pl.ds(pl.multiple_of(base, self.size), self.size), self.span(part)]
 
     def own_part(self):
-        half = self.rows // 2
-        start = pl.multiple_of(self.place["core"] * half, half)
-        return self.shard.at[pl.ds(start, half)]
+        return self.shard.at[pl.ds(pl.multiple_of(self.base, self.size), self.size), self.span(None)]
 
     def at(self, step1, step2):
         p = self.place
@@ -65,10 +74,19 @@
         target = self.at(way, 0) if dim == 1 else self.at(0, way)
         self.copy(src, dst, slot, self.place["clip"], target)
 
-    def push(self, src, dst):
-        self.copy(src, dst, 20, self.place["partner"], self.place["tm"])
-
-    OFFSETS = (0, -1, 1, 2)
+    def share(self, event):
+        index = self.at(*self.EVENTS[event])
+        whole = self.part(index)
+        self.copy(whole, whole, 20, self.place["partner"], self.place["tm"])
+        if self.split:
+            for side in (0, 1):
+                half = self.part(index, side)
+                self.copy(half, half, 21 + event, self.place["above" if side == 0 else "below"], self.place["tm"])
+
+    def lift(self, event):
+        whole = self.part(self.at(*self.EVENTS[event]), base=self.other)
+        self.arrived(whole, 21 + event)
+        self.copy(whole, whole, 20, self.place["partner"], self.place["tm"])
 
     def second_dim(self, k):
         index = self.at(self.OFFSETS[k], 0)
@@ -76,7 +94,7 @@
         self.along(2, 1, src, self.part(index), 4 + 2 * k)
         self.along(2, -1, src, self.part(index), 5 + 2 * k)
         if k > 0:
-            self.push(self.part(index), self.part(index))
+            self.share(k - 1)
 
     def own(self):
         mine = self.part(self.place["tm"])
@@ -104,24 +122,22 @@
         low, high = self.at(step, -1), self.at(step, 1)
         self.arrived(self.part(low), 4 + 2 * k)
         self.along(2, 1, self.part(low, 0), self.part(low, 0), 12 + 2 * k)
-        self.push(self.part(low), self.part(low))
+        self.share(3 + 2 * k)
         self.arrived(self.part(high), 5 + 2 * k)
         self.along(2, -1, self.part(high, 1), self.part(high, 1), 13 + 2 * k)
-        self.push(self.part(high), self.part(high))
+        self.share(4 + 2 * k)
 
     def second_far(self, k):
         far = self.at(self.OFFSETS[k], 2)
         self.arrived(self.part(far, 0), 12 + 2 * k)
         self.arrived(self.part(far, 1), 13 + 2 * k)
-        self.push(self.part(far), self.part(far))
+        self.share(11 + k)
 
     def pushed(self):
-        half = self.rows // 2
-        ref = self.full.at[pl.ds(0, TM - 1), pl.ds(0, half)]
-        self.arrived(ref, 20)
+        self.arrived(self.full.at[pl.ds(0, TM - 1), pl.ds(0, self.rows // 2), self.span(None)], 20)
 
     def drained(self):
-        ref = self.full.at[pl.ds(0, TM - 1)]
+        ref = self.full.at[pl.ds(0, TM - 1), :, self.span(None)]
         pltpu.make_async_copy(ref, ref, self.send).wait()
 
 
@@ -136,26 +152,22 @@
     lax.fori_loop(0, ref.shape[0] // 32, step, 0)
 
 
-def attend(queries, keys, values, out, bias, heads):
-    scale = 1.0 / math.sqrt(HD)
-
-    def step(index, carry):
-        for head in (2 * index, 2 * index + 1):
-            cols = pl.ds(pl.multiple_of(head * HD, HD), HD)
-            scores = lax.dot_general(
-                queries[:, cols], keys[:, cols], (((1,), (1,)), ((), ())), preferred_element_type=jnp.float32
-            )
-            scores = scores * scale
-            if bias is not None:
-                scores = jnp.where(bias[...] > 0.5, scores, MASKED)
-            top = jnp.max(scores, axis=-1, keepdims=True)
-            terms = jnp.exp(scores - top)
-            weights = (terms * (1.0 / jnp.sum(terms, axis=-1, keepdims=True))).astype(jnp.bfloat16)
-            mixed = jnp.dot(weights, values[:, cols], preferred_element_type=jnp.float32)
-            out[:, cols] = mixed.astype(jnp.bfloat16)
-        return carry
-
-    lax.fori_loop(0, heads // 2, step, 0)
+def head_weights(queries, keys, head, bias):
+    cols = pl.ds(pl.multiple_of(head * HD, HD), HD)
+    scores = lax.dot_general(
+        queries[:, cols], keys[:, cols], (((1,), (1,)), ((), ())), preferred_element_type=jnp.float32
+    )
+    scores = scores * (1.0 / math.sqrt(HD))
+    if bias is not None:
+        scores = jnp.where(bias[...] > 0.5, scores, MASKED)
+    terms = jnp.exp(scores - jnp.max(scores, axis=-1, keepdims=True))
+    return (terms * (1.0 / jnp.sum(terms, axis=-1, keepdims=True))).astype(jnp.bfloat16)
+
+
+def head_mix(weights, values, out, head):
+    cols = pl.ds(pl.multiple_of(head * HD, HD), HD)
+    mixed = jnp.dot(weights, values[:, cols], preferred_element_type=jnp.float32)
+    out[:, cols] = mixed.astype(jnp.bfloat16)
 
 
 def layer_kernel(
@@ -163,8 +175,8 @@
     out,
     tok_v, mixed_v, normed_v, spread_v, qkv_v, home_v, allowed_v, mask_v, ids_v, gates_v,
     proj_s, qkv_w, proj_t, gate_w, up_w, down_w, outgoing, received, answers, hidden_v, total_v,
-    slots_v, slots_t,
-    local_sem, send_sem, recv_s, recv_q, recv_t, swap_send, swap_recv, moe_send, go_recv, back_recv,
+    cols_v, slots_t, weights_v,
+    local_sem, send_sem, recv_s, recv_q, recv_v, recv_t, swap_send, swap_recv, moe_send, go_recv, back_recv,
 ):
     clip = lax.axis_index("clip")
     tm = lax.axis_index("tm")
@@ -183,10 +195,16 @@
         "i2": y * (1 - core) + x * core,
         "s1": 1 + 3 * core,
         "s2": 4 - 3 * core,
+        "parity": lax.rem(clip // 2, 2),
+        "above": lax.rem(clip + 2, DEVICES // TM),
+        "below": lax.rem(clip + DEVICES // TM - 2, DEVICES // TM),
     }
-    spatial = Gather(sproj, proj_s, place, send_sem.at[0], recv_s)
-    qkv = Gather(tqkv, qkv_w, place, send_sem.at[1], recv_q)
-    temporal = Gather(tproj, proj_t, place, send_sem.at[2], recv_t)
+    model = tok_v.shape[1]
+    width = 512
+    spatial = Gather(sproj, proj_s, 0, model, place, send_sem.at[0], recv_s, False)
+    scored = Gather(tqkv, qkv_w, 0, 2 * head_width, place, send_sem.at[1], recv_q, True)
+    valued = Gather(tqkv, qkv_w, 2 * head_width, head_width, place, send_sem.at[2], recv_v, True)
+    temporal = Gather(tproj, proj_t, 0, model, place, send_sem.at[3], recv_t, True)
 
     loads = [
         pltpu.make_async_copy(src, dst, local_sem.at[n])
@@ -217,30 +235,33 @@
     pl.semaphore_wait(barrier, DEVICES - 1)
 
     spatial.own()
-    qkv.own()
+    scored.own()
 
     for n in (0, 1, 2):
         loads[n].wait()
     triple_of = [qkv_v.at[:, pl.ds(n * head_width, head_width)] for n in range(3)]
-    attend(*triple_of, mixed_v, None, HEADS)
+
+    def mix_space(index, carry):
+        for head in (2 * index, 2 * index + 1):
+            head_mix(head_weights(triple_of[0], triple_of[1], head, None), triple_of[2], mixed_v, head)
+        return carry
+
+    lax.fori_loop(0, HEADS // 2, mix_space, 0)
     for load in loads[10:]:
         load.start()
 
     spatial.first_near()
     spatial.first_far()
-    qkv.first_near()
-    temporal.own()
+    scored.first_near()
     for k in range(4):
         spatial.second_near(k)
+    scored.first_far()
     for k in range(4):
         spatial.second_far(k)
-    qkv.first_far()
+    valued.own()
     loads[3].wait()
     loads[4].wait()
     spatial.pushed()
-
-    model = tok_v.shape[1]
-    width = 512
 
     def project(chunk, carry):
         cols = pl.ds(pl.multiple_of(chunk * width, width), width)
@@ -280,12 +301,17 @@
 
     kept = swap(block_of(normed_v), spread_v, 0)
 
-    temporal.first_near()
+    for event in (0, 1, 2):
+        scored.lift(event)
     for k in range(4):
-        qkv.second_near(k)
-    temporal.first_far()
+        scored.second_near(k)
+    valued.first_near()
+    valued.first_far()
     for k in range(4):
-        qkv.second_far(k)
+        scored.second_far(k)
+    temporal.own()
+    for event in range(3, 15):
+        scored.lift(event)
 
     rows = lax.broadcasted_iota(jnp.int32, (positions, TM), 0) // per
     cols16 = lax.broadcasted_iota(jnp.int32, (positions, TM), 1)
@@ -298,10 +324,10 @@
     pos_c = lax.rem(lax.broadcasted_iota(jnp.int32, (positions, positions), 1), per)
     allowed_v[...] = jnp.where(pos_r == pos_c, pairs, 0.0)
 
-    number_slots(ids_v, slots_v, slots_t, loads[8], clip, tm)
+    number_slots(ids_v, gates_v, cols_v, slots_t, loads[8:10], clip, tm)
 
     loads[5].wait()
-    qkv.pushed()
+    scored.pushed()
     swapped(spread_v, kept, 0)
 
     def triple(chunk):
@@ -310,15 +336,46 @@
         rows_in = spread_v[...].reshape(positions, model)
         qkv_v[:, cols] = jnp.dot(rows_in, weights, preferred_element_type=jnp.float32).astype(jnp.bfloat16)
 
-    for chunk in range(3 * head_width // width):
+    for chunk in range(2 * head_width // width):
         triple(chunk)
-        if chunk < 4:
-            temporal.second_near(chunk)
-
-    attend(*triple_of, mixed_v, allowed_v, HEADS)
+        valued.second_near(chunk)
+
+    def weigh(index, carry):
+        for head in (2 * index, 2 * index + 1):
+            weights_v[head] = head_weights(triple_of[0], triple_of[1], head, allowed_v)
+        return carry
+
+    temporal.first_near()
+    for event in (0, 1, 2, 3, 4):
+        valued.lift(event)
+    lax.fori_loop(0, HEADS // 4, weigh, 0)
+    temporal.first_far()
+    for k in range(4):
+        valued.second_far(k)
+    lax.fori_loop(HEADS // 4, HEADS // 2, weigh, 0)
+    for event in range(5, 15):
+        valued.lift(event)
+    temporal.second_near(0)
+    temporal.second_near(1)
+    valued.pushed()
+    for chunk in range(2 * head_width // width, 3 * head_width // width):
+        triple(chunk)
+
+    def mix_time(index, carry):
+        for head in (2 * index, 2 * index + 1):
+            head_mix(weights_v[head], triple_of[2], mixed_v, head)
+        return carry
+
+    lax.fori_loop(0, HEADS // 2, mix_time, 0)
     kept = swap(block_of(mixed_v), home_v, 1)
+    temporal.second_near(2)
+    temporal.second_near(3)
+    for event in range(7):
+        temporal.lift(event)
     for k in range(4):
         temporal.second_far(k)
+    for event in range(7, 15):
+        temporal.lift(event)
     loads[6].wait()
     temporal.pushed()
     swapped(home_v, kept, 1)
@@ -393,7 +450,7 @@
 
     lax.fori_loop(0, GROUPS, build, 0)
     pltpu.make_async_copy(outgoing.at[0], received.at[0], go_recv.at[0]).start()
-    for load in loads[9:]:
+    for load in loads[10:]:
         load.wait()
 
     def serve(group, carry):
@@ -440,14 +497,14 @@
         landed(group, answers, back_recv)
         lanes = lax.broadcasted_iota(jnp.int32, (positions, slots), 1) + group * slots
         picks = [
-            (lanes == slots_v[:, k : k + 1]).astype(jnp.float32).astype(jnp.bfloat16) for k in range(TOP)
+            (lanes == cols_v[:, k : k + 1].astype(jnp.int32)).astype(jnp.float32).astype(jnp.bfloat16) for k in range(TOP)
         ]
         for chunk in range(model // width):
             cols = pl.ds(chunk * width, width)
             wide = answers[pl.ds(group * size, size), :, cols].astype(jnp.float32)
             rows_in = wide.reshape(slots, width).astype(jnp.bfloat16)
             parts = [
-                jnp.dot(picks[k], rows_in, preferred_element_type=jnp.float32) * gates_v[:, k : k + 1]
+                jnp.dot(picks[k], rows_in, preferred_element_type=jnp.float32) * cols_v[:, TOP + k : TOP + k + 1]
                 for k in range(TOP)
             ]
             part = parts[0] + parts[1]
@@ -475,7 +532,8 @@
     ref = mixed_v.at[pl.ds(0, positions - per)]
     pltpu.make_async_copy(ref, ref, swap_send.at[1]).wait()
     spatial.drained()
-    qkv.drained()
+    scored.drained()
+    valued.drained()
     temporal.drained()
     ref = outgoing.at[pl.ds(0, DEVICES - 1)]
     pltpu.make_async_copy(ref, ref, moe_send.at[0]).wait()
@@ -483,26 +541,30 @@
     put.wait()
 
 
-def number_slots(ids_v, slots_v, slots_t, load, clip, tm):
-    load.wait()
-    positions = ids_v.shape[0]
-    expert = lax.broadcasted_iota(jnp.int32, (positions, DEVICES), 1)
+def number_slots(ids_v, gates_v, cols_v, slots_t, loads, clip, tm):
+    for load in loads:
+        load.wait()
+    positions = ids_v.shape[1]
+    expert = lax.broadcasted_iota(jnp.int32, (DEVICES, positions), 0)
     e_clip, e_tm = expert // TM, lax.rem(expert, TM)
     dz = lax.rem(e_clip // 2 - clip // 2 + 4, 4)
     dc = lax.rem(lax.rem(e_clip, 2) - lax.rem(clip, 2) + 2, 2)
     dy = lax.rem(e_tm // SIDE - tm // SIDE + 4, 4)
     dx = lax.rem(lax.rem(e_tm, SIDE) - lax.rem(tm, SIDE) + 4, 4)
     order = lax.rem((dz + 4 * dc + 8 * dy + 32 * dx) * INVERSE, DEVICES)
-    named = [(ids_v[:, k : k + 1] == expert).astype(jnp.float32) for k in range(TOP)]
+    named = [(ids_v[k : k + 1, :] == expert).astype(jnp.float32) for k in range(TOP)]
     rows = lax.broadcasted_iota(jnp.int32, (positions, positions), 0)
     cols = lax.broadcasted_iota(jnp.int32, (positions, positions), 1)
-    before = (cols < rows).astype(jnp.float32).astype(jnp.bfloat16)
-    counts = jnp.dot(before, (named[0] + named[1]).astype(jnp.bfloat16), preferred_element_type=jnp.float32)
+    before = (rows < cols).astype(jnp.float32).astype(jnp.bfloat16)
+    counts = jnp.dot((named[0] + named[1]).astype(jnp.bfloat16), before, preferred_element_type=jnp.float32)
     row = (order * CAP).astype(jnp.float32) + counts
-    found = [jnp.sum(named[k] * row, axis=1, keepdims=True) for k in range(TOP)]
-    table = jnp.where(expert == 0, found[0], jnp.where(expert == 1, found[1], -1.0))
-    slots_v[...] = table.astype(jnp.int32)
-    slots_t[...] = table.T.astype(jnp.int32)
+    table = jnp.zeros((DEVICES, positions), jnp.float32)
+    for k in range(TOP):
+        found = jnp.sum(named[k] * row, axis=0, keepdims=True)
+        slots_t[k : k + 1, :] = found.astype(jnp.int32)
+        table = jnp.where(expert == k, found, table)
+        table = jnp.where(expert == TOP + k, gates_v[k : k + 1, :], table)
+    cols_v[...] = table.T
 
 
 def layer(tokens, sq, sk, sv, sproj, tqkv, tproj, mask, ids, gates, w_gate, w_up, w_down):
@@ -523,13 +585,14 @@
             vm(positions, model), vm(positions, head_width), vm(positions, model), vm(TM, per, model),
             vm(positions, 3 * head_width), vm(TM, per, head_width),
             pltpu.VMEM((positions, positions), jnp.float32), pltpu.VMEM((TM, TM), jnp.int32),
-            pltpu.VMEM((positions, TOP), jnp.int32), pltpu.VMEM((positions, TOP), jnp.float32),
+            pltpu.VMEM((TOP, positions), jnp.int32), pltpu.VMEM((TOP, positions), jnp.float32),
             vm(TM, sproj.shape[0], model), vm(TM, tqkv.shape[0], 3 * head_width), vm(TM, tproj.shape[0], model),
             vm(model, hidden), vm(model, hidden), vm(hidden, model),
             vm(DEVICES, CAP, model), vm(DEVICES, CAP, model), vm(DEVICES, CAP, model),
             vm(positions, hidden), pltpu.VMEM((positions, model), jnp.float32),
-            pltpu.VMEM((positions, DEVICES), jnp.int32), pltpu.VMEM((DEVICES, positions), jnp.int32),
-            dma(16), dma(3), dma(21), dma(21), dma(21), dma(2), dma(2), dma(2), dma(GROUPS), dma(GROUPS),
+            pltpu.VMEM((positions, DEVICES), jnp.float32), pltpu.VMEM((8, positions), jnp.int32),
+            vm(HEADS, positions, positions),
+            dma(16), dma(4), dma(36), dma(36), dma(36), dma(36), dma(2), dma(2), dma(2), dma(GROUPS), dma(GROUPS),
         ],
         compiler_params=pltpu.CompilerParams(
             collective_id=0, has_side_effects=True, vmem_limit_bytes=67043328
@@ -563,8 +626,8 @@
         temporal_qkv,
         temporal_proj,
         frame_mask.reshape(frame_mask.shape[1:]),
-        expert_ids.reshape(positions, TOP),
-        gate_values.reshape(positions, TOP),
+        expert_ids.reshape(positions, TOP).T,
+        gate_values.reshape(positions, TOP).T,
         expert_gate[0],
         expert_up[0],
         expert_down[0],

time: 202 us -> 205 us (1.015)
  the two profiles are of different devices: /device:TPU:1 before, /device:TPU:56 now
where the time goes in v3:
time: 205 us; the launch traced here: 204 us
  Pallas kernels  202 us (99%)
  local copies, waits for them, and re-layouts  2.3 us (1%)
    pallas_call x1, Pallas kernels, layer(): pl.pallas_call(layer_kernel, out_shape=jax.ShapeDtypeStruct((positions, m...  202 us

profile of v3, /device:TPU:56, one launch (start us, length us, event | category | flops | bytes accessed | tf_op | source)
XLA Modules:
  0.0 204.5 jit_solution(1873687496636990888)
XLA Ops:
  0.0 202.2 %layer.1 = bf16[256,2048]{1,0:T(8,128)(2,1)} custom-call(bf16[256,2048]{1,0:T(8,128)(2,1)} %bitcast.19, bf16[256,1024]{1,0:T(8,128)(2,1)} %bitcast.20, bf16[256,1024]{1,0:T(8,128)(2,1)} %bitcast.21, bf16[256,1024]{1,0:T(8,128)(2,1)} %bitcast.22, bf16[64,2048]{1,0:T(8,128)(2,1)} %sproj.1, bf16[128,3072]{1,0:T(8,128)(2,1)} %tqkv.1, bf16[64,2048]{1,0:T(8,128)(2,1)} %tproj.1, ...), custom_call_target="tpu_custom_call" | custom-call | tf_op jit(solution)/shard_map/layer/pallas_call | solution.py:579
  202.2 2.3 %copy.15 = bf16[1,1,256,2048]{3,2,1,0:T(8,128)(2,1)} copy(bf16[1,1,256,2048]{3,2,1,0:T(8,128)(2,1)} %bitcast.18) | data formatting | bytes 2097152

commit v4 on v3

--- a/solution.py
+++ b/solution.py
@@ -204,7 +204,7 @@
     spatial = Gather(sproj, proj_s, 0, model, place, send_sem.at[0], recv_s, False)
     scored = Gather(tqkv, qkv_w, 0, 2 * head_width, place, send_sem.at[1], recv_q, True)
     valued = Gather(tqkv, qkv_w, 2 * head_width, head_width, place, send_sem.at[2], recv_v, True)
-    temporal = Gather(tproj, proj_t, 0, model, place, send_sem.at[3], recv_t, True)
+    temporal = Gather(tproj, proj_t, 0, model, place, send_sem.at[3], recv_t, False)
 
     loads = [
         pltpu.make_async_copy(src, dst, local_sem.at[n])
@@ -224,14 +224,12 @@
 
     barrier = pltpu.get_barrier_semaphore()
 
-    def greet(step, carry):
-        other = lax.rem(me + step, DEVICES)
+    clips = [lax.rem(clip + n, DEVICES // TM) for n in range(DEVICES // TM)]
+    tms = [lax.rem(tm + n, TM) for n in range(TM)]
+    for n in range(1, DEVICES):
         pl.semaphore_signal(
-            barrier, inc=1, device_id=(other // TM, lax.rem(other, TM)), device_id_type=MESH
+            barrier, inc=1, device_id=(clips[n // TM], tms[n % TM]), device_id_type=MESH
         )
-        return carry
-
-    lax.fori_loop(1, DEVICES, greet, 0)
     pl.semaphore_wait(barrier, DEVICES - 1)
 
     spatial.own()
@@ -251,14 +249,41 @@
         load.start()
 
     spatial.first_near()
+    spatial.second_near(0)
+    scored.first_near()
+    scored.second_near(0)
     spatial.first_far()
-    scored.first_near()
-    for k in range(4):
-        spatial.second_near(k)
+    spatial.second_near(1)
     scored.first_far()
-    for k in range(4):
-        spatial.second_far(k)
+    scored.lift(0)
+    spatial.second_near(2)
+    scored.lift(1)
+    spatial.second_far(0)
+    scored.lift(3)
+    scored.second_near(1)
     valued.own()
+    scored.lift(4)
+    scored.second_near(2)
+    scored.second_far(0)
+    scored.lift(2)
+    valued.first_near()
+    scored.lift(5)
+    spatial.second_near(3)
+    spatial.second_far(1)
+    scored.lift(6)
+    valued.first_far()
+    scored.second_near(3)
+    scored.lift(7)
+    spatial.second_far(2)
+    scored.second_far(1)
+    scored.lift(8)
+    valued.second_near(0)
+    scored.second_far(2)
+    valued.second_near(1)
+    valued.second_near(2)
+    spatial.second_far(3)
+    valued.second_near(3)
+    temporal.own()
     loads[3].wait()
     loads[4].wait()
     spatial.pushed()
@@ -301,17 +326,13 @@
 
     kept = swap(block_of(normed_v), spread_v, 0)
 
+    scored.second_far(3)
+    for k in range(4):
+        valued.second_far(k)
+    for event in (11, 9, 10, 12):
+        scored.lift(event)
     for event in (0, 1, 2):
-        scored.lift(event)
-    for k in range(4):
-        scored.second_near(k)
-    valued.first_near()
-    valued.first_far()
-    for k in range(4):
-        scored.second_far(k)
-    temporal.own()
-    for event in range(3, 15):
-        scored.lift(event)
+        valued.lift(event)
 
     rows = lax.broadcasted_iota(jnp.int32, (positions, TM), 0) // per
     cols16 = lax.broadcasted_iota(jnp.int32, (positions, TM), 1)
@@ -326,6 +347,16 @@
 
     number_slots(ids_v, gates_v, cols_v, slots_t, loads[8:10], clip, tm)
 
+    temporal.first_near()
+    temporal.second_near(0)
+    valued.lift(3)
+    valued.lift(4)
+    scored.lift(13)
+    for event in range(5, 11):
+        valued.lift(event)
+    scored.lift(14)
+    for event in range(11, 15):
+        valued.lift(event)
     loads[5].wait()
     scored.pushed()
     swapped(spread_v, kept, 0)
@@ -338,28 +369,24 @@
 
     for chunk in range(2 * head_width // width):
         triple(chunk)
-        valued.second_near(chunk)
+        if chunk == 2:
+            temporal.first_far()
+            temporal.second_near(1)
 
     def weigh(index, carry):
         for head in (2 * index, 2 * index + 1):
             weights_v[head] = head_weights(triple_of[0], triple_of[1], head, allowed_v)
         return carry
 
-    temporal.first_near()
-    for event in (0, 1, 2, 3, 4):
-        valued.lift(event)
     lax.fori_loop(0, HEADS // 4, weigh, 0)
-    temporal.first_far()
-    for k in range(4):
-        valued.second_far(k)
+    temporal.second_near(2)
     lax.fori_loop(HEADS // 4, HEADS // 2, weigh, 0)
-    for event in range(5, 15):
-        valued.lift(event)
-    temporal.second_near(0)
-    temporal.second_near(1)
+    temporal.second_far(0)
     valued.pushed()
     for chunk in range(2 * head_width // width, 3 * head_width // width):
         triple(chunk)
+    temporal.second_far(1)
+    temporal.second_near(3)
 
     def mix_time(index, carry):
         for head in (2 * index, 2 * index + 1):
@@ -368,14 +395,8 @@
 
     lax.fori_loop(0, HEADS // 2, mix_time, 0)
     kept = swap(block_of(mixed_v), home_v, 1)
-    temporal.second_near(2)
-    temporal.second_near(3)
-    for event in range(7):
-        temporal.lift(event)
-    for k in range(4):
-        temporal.second_far(k)
-    for event in range(7, 15):
-        temporal.lift(event)
+    temporal.second_far(2)
+    temporal.second_far(3)
     loads[6].wait()
     temporal.pushed()
     swapped(home_v, kept, 1)
@@ -398,34 +419,30 @@
     size = DEVICES // GROUPS
     slots = size * CAP
 
-    def peer(order, sign):
-        offset = lax.rem(order * STRIDE, DEVICES)
-        dz, dc = lax.rem(offset, 4), lax.rem(offset // 4, 2)
-        dy, dx = lax.rem(offset // 8, 4), offset // 32
-        to_z = lax.rem(clip // 2 + sign * dz + 4, 4)
-        to_c = lax.rem(core + dc, 2)
-        to_y = lax.rem(y + sign * dy + 4, 4)
-        to_x = lax.rem(x + sign * dx + 4, 4)
-        return to_z * 2 + to_c, to_y * 4 + to_x
-
     def ship(group, sign, src, dst, sends, receives):
-        def step(order, carry):
-            to_clip, to_tm = peer(order, sign)
-
-            @pl.when(order > 0)
-            def _():
-                pltpu.make_async_remote_copy(
-                    src_ref=src.at[order],
-                    dst_ref=dst.at[order],
-                    send_sem=sends,
-                    recv_sem=receives.at[group],
-                    device_id=(to_clip, to_tm),
-                    device_id_type=MESH,
-                ).start()
-
-            return carry
-
-        lax.fori_loop(group * size, group * size + size, step, 0)
+        to_clip = [
+            lax.rem(clip // 2 + sign * dz + 4, 4) * 2 + lax.rem(core + dc, 2) for dc in range(2) for dz in range(4)
+        ]
+        to_y = [lax.rem(y + sign * dy + 4, 4) * 4 for dy in range(4)]
+        to_x = [lax.rem(x + sign * (dx + group) + 8, 4) for dx in range(4)]
+        to_tm = [row + col for col in to_x for row in to_y]
+
+        def send(message, offset):
+            pltpu.make_async_remote_copy(
+                src_ref=src.at[group * size + message],
+                dst_ref=dst.at[group * size + message],
+                send_sem=sends,
+                recv_sem=receives.at[group],
+                device_id=(to_clip[offset % 8], to_tm[offset // 8]),
+                device_id_type=MESH,
+            ).start()
+
+        @pl.when(group > 0)
+        def _():
+            send(0, 0)
+
+        for message in range(1, size):
+            send(message, message * STRIDE % DEVICES)
 
     def landed(group, dst, receives):
         ref = dst.at[pl.ds(0, size)]
@@ -493,11 +510,12 @@
 
     lax.fori_loop(0, GROUPS, serve, 0)
 
-    def combine(group, carry):
+    def answered(group, finish):
         landed(group, answers, back_recv)
         lanes = lax.broadcasted_iota(jnp.int32, (positions, slots), 1) + group * slots
         picks = [
-            (lanes == cols_v[:, k : k + 1].astype(jnp.int32)).astype(jnp.float32).astype(jnp.bfloat16) for k in range(TOP)
+            (lanes == cols_v[:, k : k + 1].astype(jnp.int32)).astype(jnp.float32).astype(jnp.bfloat16)
+            for k in range(TOP)
         ]
         for chunk in range(model // width):
             cols = pl.ds(chunk * width, width)
@@ -507,28 +525,29 @@
                 jnp.dot(picks[k], rows_in, preferred_element_type=jnp.float32) * cols_v[:, TOP + k : TOP + k + 1]
                 for k in range(TOP)
             ]
-            part = parts[0] + parts[1]
-
-            @pl.when(group == 0)
-            def _():
-                total_v[:, cols] = part
-
-            @pl.when(group > 0)
-            def _():
-                total_v[:, cols] = total_v[:, cols] + part
-
-        return carry
-
-    lax.fori_loop(0, GROUPS, combine, 0)
-
-    def close(block, carry):
-        rows_at = pl.ds(pl.multiple_of(block * 32, 32), 32)
-        tok_v[rows_at, :] = (tok_v[rows_at, :].astype(jnp.float32) + total_v[rows_at, :]).astype(jnp.bfloat16)
-        return carry
-
-    lax.fori_loop(0, positions // 32, close, 0)
-    put = pltpu.make_async_copy(tok_v, out, local_sem.at[15])
-    put.start()
+            finish(chunk, cols, parts[0] + parts[1])
+
+    def begin(chunk, cols, part):
+        total_v[:, cols] = tok_v[:, cols].astype(jnp.float32) + part
+
+    def extend(chunk, cols, part):
+        total_v[:, cols] = total_v[:, cols] + part
+
+    puts = []
+
+    def close(chunk, cols, part):
+        tok_v[:, cols] = (total_v[:, cols] + part).astype(jnp.bfloat16)
+        put = pltpu.make_async_copy(tok_v.at[:, cols], out.at[:, cols], local_sem.at[15 + chunk])
+        put.start()
+        puts.append(put)
+
+    def combine(group, carry):
+        answered(group, extend)
+        return carry
+
+    answered(0, begin)
+    lax.fori_loop(1, GROUPS - 1, combine, 0)
+    answered(GROUPS - 1, close)
     ref = mixed_v.at[pl.ds(0, positions - per)]
     pltpu.make_async_copy(ref, ref, swap_send.at[1]).wait()
     spatial.drained()
@@ -538,7 +557,8 @@
     ref = outgoing.at[pl.ds(0, DEVICES - 1)]
     pltpu.make_async_copy(ref, ref, moe_send.at[0]).wait()
     pltpu.make_async_copy(ref, ref, moe_send.at[1]).wait()
-    put.wait()
+    for put in puts:
+        put.wait()
 
 
 def number_slots(ids_v, gates_v, cols_v, slots_t, loads, clip, tm):
@@ -592,7 +612,7 @@
             vm(positions, hidden), pltpu.VMEM((positions, model), jnp.float32),
             pltpu.VMEM((positions, DEVICES), jnp.float32), pltpu.VMEM((8, positions), jnp.int32),
             vm(HEADS, positions, positions),
-            dma(16), dma(4), dma(36), dma(36), dma(36), dma(36), dma(2), dma(2), dma(2), dma(GROUPS), dma(GROUPS),
+            dma(19), dma(4), dma(36), dma(36), dma(36), dma(36), dma(2), dma(2), dma(2), dma(GROUPS), dma(GROUPS),
         ],
         compiler_params=pltpu.CompilerParams(
             collective_id=0, has_side_effects=True, vmem_limit_bytes=67043328

time: 205 us -> 176 us (0.86)
  the two profiles are of different devices: /device:TPU:56 before, /device:TPU:1 now
where the time goes in v4:
time: 176 us
  Pallas kernels  173 us (98%)
  local copies, waits for them, and re-layouts  2.3 us (1%)
    pallas_call x1, Pallas kernels, layer(): pl.pallas_call(layer_kernel, out_shape=jax.ShapeDtypeStruct((positions, m...  173 us

profile of v4, /device:TPU:1, one launch (start us, length us, event | category | flops | bytes accessed | tf_op | source)
XLA Modules:
  0.0 175.6 jit_solution(15875095715442561007)
XLA Ops:
  0.0 173.3 %layer.1 = bf16[256,2048]{1,0:T(8,128)(2,1)} custom-call(bf16[256,2048]{1,0:T(8,128)(2,1)} %bitcast.19, bf16[256,1024]{1,0:T(8,128)(2,1)} %bitcast.20, bf16[256,1024]{1,0:T(8,128)(2,1)} %bitcast.21, bf16[256,1024]{1,0:T(8,128)(2,1)} %bitcast.22, bf16[64,2048]{1,0:T(8,128)(2,1)} %sproj.1, bf16[128,3072]{1,0:T(8,128)(2,1)} %tqkv.1, bf16[64,2048]{1,0:T(8,128)(2,1)} %tproj.1, ...), custom_call_target="tpu_custom_call" | custom-call | tf_op jit(solution)/shard_map/layer/pallas_call | solution.py:599
  173.3 2.3 %copy.15 = bf16[1,1,256,2048]{3,2,1,0:T(8,128)(2,1)} copy(bf16[1,1,256,2048]{3,2,1,0:T(8,128)(2,1)} %bitcast.18) | data formatting | bytes 2097152

commit v5 on v4

--- a/solution.py
+++ b/solution.py
@@ -141,17 +141,6 @@
         pltpu.make_async_copy(ref, ref, self.send).wait()
 
 
-def normed_rows(ref, out):
-    def step(block, carry):
-        rows = pl.ds(pl.multiple_of(block * 32, 32), 32)
-        wide = ref[rows, :].astype(jnp.float32)
-        inverse = lax.rsqrt(jnp.mean(wide * wide, axis=-1, keepdims=True) + EPS)
-        out[rows, :] = (wide * inverse).astype(jnp.bfloat16)
-        return carry
-
-    lax.fori_loop(0, ref.shape[0] // 32, step, 0)
-
-
 def head_weights(queries, keys, head, bias):
     cols = pl.ds(pl.multiple_of(head * HD, HD), HD)
     scores = lax.dot_general(
@@ -175,7 +164,7 @@
     out,
     tok_v, mixed_v, normed_v, spread_v, qkv_v, home_v, allowed_v, mask_v, ids_v, gates_v,
     proj_s, qkv_w, proj_t, gate_w, up_w, down_w, outgoing, received, answers, hidden_v, total_v,
-    cols_v, slots_t, weights_v,
+    cols_v, slots_t, inverse_v,
     local_sem, send_sem, recv_s, recv_q, recv_v, recv_t, swap_send, swap_recv, moe_send, go_recv, back_recv,
 ):
     clip = lax.axis_index("clip")
@@ -204,7 +193,7 @@
     spatial = Gather(sproj, proj_s, 0, model, place, send_sem.at[0], recv_s, False)
     scored = Gather(tqkv, qkv_w, 0, 2 * head_width, place, send_sem.at[1], recv_q, True)
     valued = Gather(tqkv, qkv_w, 2 * head_width, head_width, place, send_sem.at[2], recv_v, True)
-    temporal = Gather(tproj, proj_t, 0, model, place, send_sem.at[3], recv_t, False)
+    temporal = Gather(tproj, proj_t, 0, model, place, send_sem.at[3], recv_t, True)
 
     loads = [
         pltpu.make_async_copy(src, dst, local_sem.at[n])
@@ -284,55 +273,58 @@
     spatial.second_far(3)
     valued.second_near(3)
     temporal.own()
+
     loads[3].wait()
     loads[4].wait()
     spatial.pushed()
-
-    def project(chunk, carry):
-        cols = pl.ds(pl.multiple_of(chunk * width, width), width)
-        weights = proj_s[:, :, cols].reshape(mixed_v.shape[1], width)
+    squares = jnp.zeros((positions, 1), jnp.float32)
+    for chunk in range(model // width):
+        cols = pl.ds(chunk * width, width)
+        weights = proj_s[:, :, cols].reshape(head_width, width)
         update = jnp.dot(mixed_v[...], weights, preferred_element_type=jnp.float32)
-        tok_v[:, cols] = (tok_v[:, cols].astype(jnp.float32) + update).astype(jnp.bfloat16)
-        return carry
-
-    lax.fori_loop(0, model // width, project, 0)
-    normed_rows(tok_v, normed_v)
-
-    def swap(src_of, dst, slot):
-        def step(shift, carry):
-            other = lax.rem(tm + shift, TM)
+        first = (tok_v[:, cols].astype(jnp.float32) + update).astype(jnp.bfloat16)
+        tok_v[:, cols] = first
+        wide = first.astype(jnp.float32)
+        squares = squares + jnp.sum(wide * wide, axis=-1, keepdims=True)
+    inverse_v[...] = lax.rsqrt(squares * (1.0 / model) + EPS)
+
+    def block(index):
+        return pl.ds(pl.multiple_of(index * per, per), per)
+
+    def spread(shift, carry):
+        other = lax.rem(tm + shift, TM)
+        rows_at = block(other)
+        normed_v[rows_at, :] = (tok_v[rows_at, :].astype(jnp.float32) * inverse_v[rows_at, :]).astype(jnp.bfloat16)
+
+        @pl.when(shift < TM)
+        def _():
             pltpu.make_async_remote_copy(
-                src_ref=src_of(other),
-                dst_ref=dst.at[tm],
-                send_sem=swap_send.at[slot],
-                recv_sem=swap_recv.at[slot],
+                src_ref=normed_v.at[rows_at],
+                dst_ref=spread_v.at[tm],
+                send_sem=swap_send.at[0],
+                recv_sem=swap_recv.at[0],
                 device_id=(clip, other),
                 device_id_type=MESH,
             ).start()
-            return carry
-
-        lax.fori_loop(1, TM, step, 0)
-        kept = pltpu.make_async_copy(src_of(tm), dst.at[tm], local_sem.at[13 + slot])
-        kept.start()
-        return kept
-
-    def swapped(dst, kept, slot):
-        ref = dst.at[pl.ds(0, TM - 1)]
-        pltpu.make_async_copy(ref, ref, swap_recv.at[slot]).wait()
-        kept.wait()
-
-    def block_of(ref):
-        return lambda index: ref.at[pl.ds(pl.multiple_of(index * per, per), per)]
-
-    kept = swap(block_of(normed_v), spread_v, 0)
+
+        return carry
+
+    lax.fori_loop(1, TM + 1, spread, 0)
+    kept = pltpu.make_async_copy(normed_v.at[block(tm)], spread_v.at[tm], local_sem.at[13])
+    kept.start()
 
     scored.second_far(3)
-    for k in range(4):
-        valued.second_far(k)
-    for event in (11, 9, 10, 12):
-        scored.lift(event)
-    for event in (0, 1, 2):
-        valued.lift(event)
+    valued.second_far(0)
+    valued.second_far(1)
+    valued.second_far(2)
+    valued.second_far(3)
+    scored.lift(11)
+    scored.lift(9)
+    scored.lift(10)
+    scored.lift(12)
+    valued.lift(0)
+    valued.lift(1)
+    valued.lift(2)
 
     rows = lax.broadcasted_iota(jnp.int32, (positions, TM), 0) // per
     cols16 = lax.broadcasted_iota(jnp.int32, (positions, TM), 1)
@@ -344,7 +336,6 @@
     pos_r = lax.rem(lax.broadcasted_iota(jnp.int32, (positions, positions), 0), per)
     pos_c = lax.rem(lax.broadcasted_iota(jnp.int32, (positions, positions), 1), per)
     allowed_v[...] = jnp.where(pos_r == pos_c, pairs, 0.0)
-
     number_slots(ids_v, gates_v, cols_v, slots_t, loads[8:10], clip, tm)
 
     temporal.first_near()
@@ -352,69 +343,147 @@
     valued.lift(3)
     valued.lift(4)
     scored.lift(13)
-    for event in range(5, 11):
-        valued.lift(event)
+    valued.lift(5)
+    valued.lift(6)
+    valued.lift(7)
+    valued.lift(8)
+    valued.lift(9)
+    valued.lift(10)
     scored.lift(14)
-    for event in range(11, 15):
-        valued.lift(event)
+    valued.lift(11)
+    valued.lift(12)
+    valued.lift(13)
+    valued.lift(14)
+
     loads[5].wait()
     scored.pushed()
-    swapped(spread_v, kept, 0)
-
-    def triple(chunk):
-        cols = pl.ds(chunk * width, width)
-        weights = qkv_w[:, :, cols].reshape(model, width)
+    ref = spread_v.at[pl.ds(0, TM - 1)]
+    pltpu.make_async_copy(ref, ref, swap_recv.at[0]).wait()
+    kept.wait()
+
+    quarter = head_width // 4
+    homes = []
+
+    def triple(part, number):
+        cols = pl.ds(part * head_width + number * quarter, quarter)
+        weights = qkv_w[:, :, cols].reshape(model, quarter)
         rows_in = spread_v[...].reshape(positions, model)
         qkv_v[:, cols] = jnp.dot(rows_in, weights, preferred_element_type=jnp.float32).astype(jnp.bfloat16)
 
-    for chunk in range(2 * head_width // width):
-        triple(chunk)
-        if chunk == 2:
-            temporal.first_far()
-            temporal.second_near(1)
-
-    def weigh(index, carry):
-        for head in (2 * index, 2 * index + 1):
-            weights_v[head] = head_weights(triple_of[0], triple_of[1], head, allowed_v)
-        return carry
-
-    lax.fori_loop(0, HEADS // 4, weigh, 0)
+    def score_part(number):
+        triple(0, number)
+        triple(1, number)
+        return [
+            head_weights(triple_of[0], triple_of[1], head, allowed_v) for head in (2 * number, 2 * number + 1)
+        ]
+
+    def value_part(number, weights):
+        triple(2, number)
+        for n in range(2):
+            head_mix(weights[n], triple_of[2], mixed_v, 2 * number + n)
+        cols = pl.ds(number * quarter, quarter)
+
+        def send(shift, carry):
+            other = lax.rem(tm + shift, TM)
+            pltpu.make_async_remote_copy(
+                src_ref=mixed_v.at[block(other), cols],
+                dst_ref=home_v.at[tm, :, cols],
+                send_sem=swap_send.at[1],
+                recv_sem=swap_recv.at[1 + number],
+                device_id=(clip, other),
+                device_id_type=MESH,
+            ).start()
+            return carry
+
+        lax.fori_loop(1, TM, send, 0)
+        home = pltpu.make_async_copy(mixed_v.at[block(tm), cols], home_v.at[tm, :, cols], local_sem.at[19 + number])
+        home.start()
+        homes.append(home)
+
+    weights = score_part(0)
+
+    valued.pushed()
+    value_part(0, weights)
+
+    temporal.first_far()
+    temporal.second_near(1)
+
+    weights = score_part(1)
+
+    value_part(1, weights)
+
     temporal.second_near(2)
-    lax.fori_loop(HEADS // 4, HEADS // 2, weigh, 0)
+
+    weights = score_part(2)
+
+    value_part(2, weights)
+
     temporal.second_far(0)
-    valued.pushed()
-    for chunk in range(2 * head_width // width, 3 * head_width // width):
-        triple(chunk)
     temporal.second_far(1)
     temporal.second_near(3)
 
-    def mix_time(index, carry):
-        for head in (2 * index, 2 * index + 1):
-            head_mix(weights_v[head], triple_of[2], mixed_v, head)
-        return carry
-
-    lax.fori_loop(0, HEADS // 2, mix_time, 0)
-    kept = swap(block_of(mixed_v), home_v, 1)
+    weights = score_part(3)
+
+    value_part(3, weights)
+
     temporal.second_far(2)
     temporal.second_far(3)
+    temporal.lift(0)
+    temporal.lift(1)
+    temporal.lift(2)
+    temporal.lift(3)
+    temporal.lift(4)
+    temporal.lift(5)
+    temporal.lift(6)
+    temporal.lift(7)
+    temporal.lift(8)
+    temporal.lift(9)
+    temporal.lift(10)
+    temporal.lift(11)
+    temporal.lift(12)
+    temporal.lift(13)
+    temporal.lift(14)
+
     loads[6].wait()
     temporal.pushed()
-    swapped(home_v, kept, 1)
-
-    def finish(chunk, carry):
-        cols = pl.ds(pl.multiple_of(chunk * width, width), width)
-        weights = proj_t[:, :, cols].reshape(head_width, width)
-        rows_in = home_v[...].reshape(positions, head_width)
-        update = jnp.dot(rows_in, weights, preferred_element_type=jnp.float32).astype(jnp.bfloat16)
-        tok_v[:, cols] = (
-            tok_v[:, cols].astype(jnp.float32) + update.astype(jnp.float32)
-        ).astype(jnp.bfloat16)
-        return carry
-
-    lax.fori_loop(0, model // width, finish, 0)
+
+    def come_home(number):
+        ref = home_v.at[pl.ds(0, TM - 1), :, pl.ds(number * quarter, quarter)]
+        pltpu.make_async_copy(ref, ref, swap_recv.at[1 + number]).wait()
+        homes[number].wait()
+
+    def back(half, cols):
+        low = half * 2 * quarter
+        weights = proj_t[half * (TM // 2) : (half + 1) * (TM // 2), :, cols].reshape(2 * quarter, width)
+        rows_in = home_v[:, :, low : low + 2 * quarter].reshape(positions, 2 * quarter)
+        return jnp.dot(rows_in, weights, preferred_element_type=jnp.float32)
+
+    come_home(0)
+    come_home(1)
+    for chunk in range(model // width):
+        cols = pl.ds(chunk * width, width)
+        total_v[:, cols] = back(0, cols)
+    come_home(2)
+    come_home(3)
+    squares = jnp.zeros((positions, 1), jnp.float32)
+    for chunk in range(model // width):
+        cols = pl.ds(chunk * width, width)
+        update = (total_v[:, cols] + back(1, cols)).astype(jnp.bfloat16)
+        second = (tok_v[:, cols].astype(jnp.float32) + update.astype(jnp.float32)).astype(jnp.bfloat16)
+        tok_v[:, cols] = second
+        wide = second.astype(jnp.float32)
+        squares = squares + jnp.sum(wide * wide, axis=-1, keepdims=True)
     ref = normed_v.at[pl.ds(0, positions - per)]
     pltpu.make_async_copy(ref, ref, swap_send.at[0]).wait()
-    normed_rows(tok_v, normed_v)
+    inverse_v[...] = lax.rsqrt(squares * (1.0 / model) + EPS)
+
+    def scale(index, carry):
+        rows_at = pl.ds(pl.multiple_of(index * 32, 32), 32)
+        normed_v[rows_at, :] = (tok_v[rows_at, :].astype(jnp.float32) * inverse_v[rows_at, :]).astype(jnp.bfloat16)
+        return carry
+
+    lax.fori_loop(0, positions // 32, scale, 0)
+
 
     size = DEVICES // GROUPS
     slots = size * CAP
@@ -611,8 +680,8 @@
             vm(DEVICES, CAP, model), vm(DEVICES, CAP, model), vm(DEVICES, CAP, model),
             vm(positions, hidden), pltpu.VMEM((positions, model), jnp.float32),
             pltpu.VMEM((positions, DEVICES), jnp.float32), pltpu.VMEM((8, positions), jnp.int32),
-            vm(HEADS, positions, positions),
-            dma(19), dma(4), dma(36), dma(36), dma(36), dma(36), dma(2), dma(2), dma(2), dma(GROUPS), dma(GROUPS),
+            pltpu.VMEM((positions, 1), jnp.float32),
+            dma(23), dma(4), dma(36), dma(36), dma(36), dma(36), dma(2), dma(5), dma(2), dma(GROUPS), dma(GROUPS),
         ],
         compiler_params=pltpu.CompilerParams(
             collective_id=0, has_side_effects=True, vmem_limit_bytes=67043328

time: 176 us -> 174 us (0.989)
  no operation moved by 1% of the time
where the time goes in v5:
time: 174 us
  Pallas kernels  172 us (99%)
  local copies, waits for them, and re-layouts  2.3 us (1%)
    pallas_call x1, Pallas kernels, layer(): pl.pallas_call(layer_kernel, out_shape=jax.ShapeDtypeStruct((positions, m...  172 us

profile of v5, /device:TPU:1, one launch (start us, length us, event | category | flops | bytes accessed | tf_op | source)
XLA Modules:
  0.0 174.0 jit_solution(12095910076106413213)
XLA Ops:
  0.0 171.7 %layer.1 = bf16[256,2048]{1,0:T(8,128)(2,1)} custom-call(bf16[256,2048]{1,0:T(8,128)(2,1)} %bitcast.19, bf16[256,1024]{1,0:T(8,128)(2,1)} %bitcast.20, bf16[256,1024]{1,0:T(8,128)(2,1)} %bitcast.21, bf16[256,1024]{1,0:T(8,128)(2,1)} %bitcast.22, bf16[64,2048]{1,0:T(8,128)(2,1)} %sproj.1, bf16[128,3072]{1,0:T(8,128)(2,1)} %tqkv.1, bf16[64,2048]{1,0:T(8,128)(2,1)} %tproj.1, ...), custom_call_target="tpu_custom_call" | custom-call | tf_op jit(solution)/shard_map/layer/pallas_call | solution.py:668
  171.7 2.3 %copy.15 = bf16[1,1,256,2048]{3,2,1,0:T(8,128)(2,1)} copy(bf16[1,1,256,2048]{3,2,1,0:T(8,128)(2,1)} %bitcast.18) | data formatting | bytes 2097152

commit v6 on v5

--- a/solution.py
+++ b/solution.py
@@ -30,8 +30,8 @@
         (i, 2) for i in (0, -1, 1, 2)
     )
 
-    def __init__(self, shard, full, start, columns, place, send, recv, split):
-        self.shard, self.full, self.send, self.recv = shard, full, send, recv
+    def __init__(self, full, start, columns, place, send, recv, split):
+        self.full, self.send, self.recv = full, send, recv
         self.start, self.columns, self.place, self.split = start, columns, place, split
         self.rows = full.shape[1]
         self.size = self.rows // 4 if split else self.rows // 2
@@ -49,9 +49,6 @@
     def part(self, index, part=None, base=None):
         base = self.base if base is None else base
         return self.full.at[index, pl.ds(pl.multiple_of(base, self.size), self.size), self.span(part)]
-
-    def own_part(self):
-        return self.shard.at[pl.ds(pl.multiple_of(self.base, self.size), self.size), self.span(None)]
 
     def at(self, step1, step2):
         p = self.place
@@ -90,7 +87,7 @@
 
     def second_dim(self, k):
         index = self.at(self.OFFSETS[k], 0)
-        src = self.own_part() if k == 0 else self.part(index)
+        src = self.part(index)
         self.along(2, 1, src, self.part(index), 4 + 2 * k)
         self.along(2, -1, src, self.part(index), 5 + 2 * k)
         if k > 0:
@@ -98,8 +95,8 @@
 
     def own(self):
         mine = self.part(self.place["tm"])
-        self.along(1, 1, self.own_part(), mine, 0)
-        self.along(1, -1, self.own_part(), mine, 1)
+        self.along(1, 1, mine, mine, 0)
+        self.along(1, -1, mine, mine, 1)
         self.second_dim(0)
 
     def first_near(self):
@@ -146,10 +143,10 @@
     scores = lax.dot_general(
         queries[:, cols], keys[:, cols], (((1,), (1,)), ((), ())), preferred_element_type=jnp.float32
     )
-    scores = scores * (1.0 / math.sqrt(HD))
+    scores = scores * (math.log2(math.e) / math.sqrt(HD))
     if bias is not None:
-        scores = jnp.where(bias[...] > 0.5, scores, MASKED)
-    terms = jnp.exp(scores - jnp.max(scores, axis=-1, keepdims=True))
+        scores = scores + bias[...]
+    terms = jnp.exp2(scores - jnp.max(scores, axis=-1, keepdims=True))
     return (terms * (1.0 / jnp.sum(terms, axis=-1, keepdims=True))).astype(jnp.bfloat16)
 
 
@@ -190,10 +187,10 @@
     }
     model = tok_v.shape[1]
     width = 512
-    spatial = Gather(sproj, proj_s, 0, model, place, send_sem.at[0], recv_s, False)
-    scored = Gather(tqkv, qkv_w, 0, 2 * head_width, place, send_sem.at[1], recv_q, True)
-    valued = Gather(tqkv, qkv_w, 2 * head_width, head_width, place, send_sem.at[2], recv_v, True)
-    temporal = Gather(tproj, proj_t, 0, model, place, send_sem.at[3], recv_t, True)
+    spatial = Gather(proj_s, 0, model, place, send_sem.at[0], recv_s, False)
+    scored = Gather(qkv_w, 0, 2 * head_width, place, send_sem.at[1], recv_q, True)
+    valued = Gather(qkv_w, 2 * head_width, head_width, place, send_sem.at[2], recv_v, True)
+    temporal = Gather(proj_t, 0, model, place, send_sem.at[3], recv_t, True)
 
     loads = [
         pltpu.make_async_copy(src, dst, local_sem.at[n])
@@ -208,8 +205,8 @@
             ]
         )
     ]
-    for load in loads[:10]:
-        load.start()
+    for n in (4, 5, 0, 1, 2, 3, 6, 7, 8, 9):
+        loads[n].start()
 
     barrier = pltpu.get_barrier_semaphore()
 
@@ -221,7 +218,9 @@
         )
     pl.semaphore_wait(barrier, DEVICES - 1)
 
+    loads[4].wait()
     spatial.own()
+    loads[5].wait()
     scored.own()
 
     for n in (0, 1, 2):
@@ -239,43 +238,44 @@
 
     spatial.first_near()
     spatial.second_near(0)
-    scored.first_near()
     scored.second_near(0)
     spatial.first_far()
+    scored.first_near()
     spatial.second_near(1)
+    valued.own()
+    spatial.second_near(2)
+    scored.lift(3)
+    spatial.second_far(0)
+    scored.lift(4)
     scored.first_far()
+    scored.second_far(0)
     scored.lift(0)
-    spatial.second_near(2)
+    valued.first_near()
+    spatial.second_near(3)
     scored.lift(1)
-    spatial.second_far(0)
-    scored.lift(3)
+    scored.lift(2)
+    valued.first_far()
     scored.second_near(1)
-    valued.own()
-    scored.lift(4)
+    scored.lift(11)
     scored.second_near(2)
-    scored.second_far(0)
-    scored.lift(2)
-    valued.first_near()
+    valued.lift(0)
+    spatial.second_far(1)
+    valued.lift(1)
+    valued.lift(2)
+    spatial.second_far(2)
     scored.lift(5)
-    spatial.second_near(3)
-    spatial.second_far(1)
+    scored.second_near(3)
+    valued.second_near(0)
+    valued.second_near(1)
     scored.lift(6)
-    valued.first_far()
-    scored.second_near(3)
-    scored.lift(7)
-    spatial.second_far(2)
-    scored.second_far(1)
-    scored.lift(8)
-    valued.second_near(0)
-    scored.second_far(2)
-    valued.second_near(1)
     valued.second_near(2)
     spatial.second_far(3)
+    scored.lift(7)
     valued.second_near(3)
+    loads[6].wait()
     temporal.own()
 
     loads[3].wait()
-    loads[4].wait()
     spatial.pushed()
     squares = jnp.zeros((positions, 1), jnp.float32)
     for chunk in range(model // width):
@@ -313,18 +313,11 @@
     kept = pltpu.make_async_copy(normed_v.at[block(tm)], spread_v.at[tm], local_sem.at[13])
     kept.start()
 
-    scored.second_far(3)
+    scored.lift(9)
+    scored.second_far(1)
     valued.second_far(0)
-    valued.second_far(1)
-    valued.second_far(2)
-    valued.second_far(3)
-    scored.lift(11)
-    scored.lift(9)
-    scored.lift(10)
-    scored.lift(12)
-    valued.lift(0)
-    valued.lift(1)
-    valued.lift(2)
+    scored.lift(8)
+    scored.second_far(2)
 
     rows = lax.broadcasted_iota(jnp.int32, (positions, TM), 0) // per
     cols16 = lax.broadcasted_iota(jnp.int32, (positions, TM), 1)
@@ -335,27 +328,40 @@
     pairs = lax.dot_general(by_row, frame_of, (((1,), (1,)), ((), ())), preferred_element_type=jnp.float32)
     pos_r = lax.rem(lax.broadcasted_iota(jnp.int32, (positions, positions), 0), per)
     pos_c = lax.rem(lax.broadcasted_iota(jnp.int32, (positions, positions), 1), per)
-    allowed_v[...] = jnp.where(pos_r == pos_c, pairs, 0.0)
+    allowed_v[...] = jnp.where(jnp.where(pos_r == pos_c, pairs, 0.0) > 0.5, 0.0, MASKED)
     number_slots(ids_v, gates_v, cols_v, slots_t, loads[8:10], clip, tm)
 
+    valued.second_far(3)
+    valued.second_far(2)
+    valued.lift(3)
+    scored.second_far(3)
+    scored.lift(10)
+    valued.second_far(1)
     temporal.first_near()
     temporal.second_near(0)
-    valued.lift(3)
     valued.lift(4)
-    scored.lift(13)
     valued.lift(5)
     valued.lift(6)
     valued.lift(7)
+    temporal.first_far()
     valued.lift(8)
     valued.lift(9)
+    temporal.second_near(1)
     valued.lift(10)
+    scored.lift(12)
+    valued.lift(11)
+    temporal.second_near(2)
+    scored.lift(13)
+    valued.lift(14)
+    valued.lift(13)
     scored.lift(14)
-    valued.lift(11)
     valued.lift(12)
-    valued.lift(13)
-    valued.lift(14)
-
-    loads[5].wait()
+    temporal.second_far(0)
+    temporal.lift(0)
+    temporal.lift(3)
+    temporal.lift(1)
+    temporal.lift(4)
+
     scored.pushed()
     ref = spread_v.at[pl.ds(0, TM - 1)]
     pltpu.make_async_copy(ref, ref, swap_recv.at[0]).wait()
@@ -401,50 +407,29 @@
         homes.append(home)
 
     weights = score_part(0)
-
+    temporal.second_near(3)
     valued.pushed()
     value_part(0, weights)
-
-    temporal.first_far()
-    temporal.second_near(1)
-
+    temporal.lift(2)
     weights = score_part(1)
-
+    temporal.second_far(1)
     value_part(1, weights)
-
-    temporal.second_near(2)
-
+    temporal.lift(6)
+    temporal.lift(5)
+    temporal.second_far(2)
     weights = score_part(2)
-
+    temporal.lift(7)
+    temporal.lift(11)
     value_part(2, weights)
-
-    temporal.second_far(0)
-    temporal.second_far(1)
-    temporal.second_near(3)
-
+    temporal.second_far(3)
+    temporal.lift(8)
     weights = score_part(3)
-
+    temporal.lift(12)
     value_part(3, weights)
-
-    temporal.second_far(2)
-    temporal.second_far(3)
-    temporal.lift(0)
-    temporal.lift(1)
-    temporal.lift(2)
-    temporal.lift(3)
-    temporal.lift(4)
-    temporal.lift(5)
-    temporal.lift(6)
-    temporal.lift(7)
-    temporal.lift(8)
     temporal.lift(9)
     temporal.lift(10)
-    temporal.lift(11)
-    temporal.lift(12)
     temporal.lift(13)
     temporal.lift(14)
-
-    loads[6].wait()
     temporal.pushed()
 
     def come_home(number):
@@ -475,15 +460,8 @@
         squares = squares + jnp.sum(wide * wide, axis=-1, keepdims=True)
     ref = normed_v.at[pl.ds(0, positions - per)]
     pltpu.make_async_copy(ref, ref, swap_send.at[0]).wait()
-    inverse_v[...] = lax.rsqrt(squares * (1.0 / model) + EPS)
-
-    def scale(index, carry):
-        rows_at = pl.ds(pl.multiple_of(index * 32, 32), 32)
-        normed_v[rows_at, :] = (tok_v[rows_at, :].astype(jnp.float32) * inverse_v[rows_at, :]).astype(jnp.bfloat16)
-        return carry
-
-    lax.fori_loop(0, positions // 32, scale, 0)
-
+    inverse = lax.rsqrt(squares * (1.0 / model) + EPS)
+    inverse_row = jnp.broadcast_to(inverse, (positions, 128)).T[0:1, :]
 
     size = DEVICES // GROUPS
     slots = size * CAP
@@ -501,7 +479,7 @@
                 src_ref=src.at[group * size + message],
                 dst_ref=dst.at[group * size + message],
                 send_sem=sends,
-                recv_sem=receives.at[group],
+                recv_sem=receives.at[group + (group // (GROUPS - 1) if sign < 0 and message >= size // 2 else 0)],
                 device_id=(to_clip[offset % 8], to_tm[offset // 8]),
                 device_id_type=MESH,
             ).start()
@@ -513,8 +491,8 @@
         for message in range(1, size):
             send(message, message * STRIDE % DEVICES)
 
-    def landed(group, dst, receives):
-        ref = dst.at[pl.ds(0, size)]
+    def landed(group, dst, receives, count=size):
+        ref = dst.at[pl.ds(0, count)]
         pltpu.make_async_copy(ref, ref, receives.at[group]).wait()
 
     def pick(group, table):
@@ -524,10 +502,11 @@
 
     def build(group, carry):
         chosen = pick(group, slots_t[0:1, :]) + pick(group, slots_t[1:2, :])
+        factor = jnp.sum(chosen * inverse_row, axis=1, keepdims=True)
         chosen = chosen.astype(jnp.bfloat16)
         for chunk in range(model // width):
             cols = pl.ds(chunk * width, width)
-            rows_out = jnp.dot(chosen, normed_v[:, cols], preferred_element_type=jnp.float32)
+            rows_out = jnp.dot(chosen, tok_v[:, cols], preferred_element_type=jnp.float32) * factor
             outgoing[pl.ds(group * size, size), :, cols] = rows_out.reshape(size, CAP, width).astype(
                 jnp.bfloat16
             )
@@ -579,17 +558,17 @@
 
     lax.fori_loop(0, GROUPS, serve, 0)
 
-    def answered(group, finish):
-        landed(group, answers, back_recv)
-        lanes = lax.broadcasted_iota(jnp.int32, (positions, slots), 1) + group * slots
+    def answered(group, low, count, finish):
+        landed(group, answers, back_recv, count)
+        lanes = lax.broadcasted_iota(jnp.int32, (positions, count * CAP), 1) + low * CAP
         picks = [
             (lanes == cols_v[:, k : k + 1].astype(jnp.int32)).astype(jnp.float32).astype(jnp.bfloat16)
             for k in range(TOP)
         ]
         for chunk in range(model // width):
             cols = pl.ds(chunk * width, width)
-            wide = answers[pl.ds(group * size, size), :, cols].astype(jnp.float32)
-            rows_in = wide.reshape(slots, width).astype(jnp.bfloat16)
+            wide = answers[pl.ds(low, count), :, cols].astype(jnp.float32)
+            rows_in = wide.reshape(count * CAP, width).astype(jnp.bfloat16)
             parts = [
                 jnp.dot(picks[k], rows_in, preferred_element_type=jnp.float32) * cols_v[:, TOP + k : TOP + k + 1]
                 for k in range(TOP)
@@ -611,12 +590,13 @@
         puts.append(put)
 
     def combine(group, carry):
-        answered(group, extend)
+        answered(group, group * size, size, extend)
         return carry
 
-    answered(0, begin)
+    answered(0, 0, size, begin)
     lax.fori_loop(1, GROUPS - 1, combine, 0)
-    answered(GROUPS - 1, close)
+    answered(GROUPS - 1, DEVICES - size, size // 2, extend)
+    answered(GROUPS, DEVICES - size // 2, size // 2, close)
     ref = mixed_v.at[pl.ds(0, positions - per)]
     pltpu.make_async_copy(ref, ref, swap_send.at[1]).wait()
     spatial.drained()
@@ -681,7 +661,7 @@
             vm(positions, hidden), pltpu.VMEM((positions, model), jnp.float32),
             pltpu.VMEM((positions, DEVICES), jnp.float32), pltpu.VMEM((8, positions), jnp.int32),
             pltpu.VMEM((positions, 1), jnp.float32),
-            dma(23), dma(4), dma(36), dma(36), dma(36), dma(36), dma(2), dma(5), dma(2), dma(GROUPS), dma(GROUPS),
+            dma(23), dma(4), dma(36), dma(36), dma(36), dma(36), dma(2), dma(5), dma(2), dma(GROUPS), dma(GROUPS + 1),
         ],
         compiler_params=pltpu.CompilerParams(
             collective_id=0, has_side_effects=True, vmem_limit_bytes=67043328

time: 174 us -> 173 us (level)
  no operation moved by 1% of the time
where the time goes in v6:
time: 173 us
  Pallas kernels  171 us (99%)
  local copies, waits for them, and re-layouts  2.3 us (1%)
    pallas_call x1, Pallas kernels, layer(): pl.pallas_call(layer_kernel, out_shape=jax.ShapeDtypeStruct((positions, m...  171 us

profile of v6, /device:TPU:1, one launch (start us, length us, event | category | flops | bytes accessed | tf_op | source)
XLA Modules:
  0.0 173.1 jit_solution(12191040687117709883)
XLA Ops:
  0.0 170.8 %layer.1 = bf16[256,2048]{1,0:T(8,128)(2,1)} custom-call(bf16[256,2048]{1,0:T(8,128)(2,1)} %bitcast.19, bf16[256,1024]{1,0:T(8,128)(2,1)} %bitcast.20, bf16[256,1024]{1,0:T(8,128)(2,1)} %bitcast.21, bf16[256,1024]{1,0:T(8,128)(2,1)} %bitcast.22, bf16[64,2048]{1,0:T(8,128)(2,1)} %sproj.1, bf16[128,3072]{1,0:T(8,128)(2,1)} %tqkv.1, bf16[64,2048]{1,0:T(8,128)(2,1)} %tproj.1, ...), custom_call_target="tpu_custom_call" | custom-call | tf_op jit(solution)/shard_map/layer/pallas_call | solution.py:648
  170.8 2.3 %copy.15 = bf16[1,1,256,2048]{3,2,1,0:T(8,128)(2,1)} copy(bf16[1,1,256,2048]{3,2,1,0:T(8,128)(2,1)} %bitcast.18) | data formatting | bytes 2097152

commit v7 on v6

--- a/solution.py
+++ b/solution.py
@@ -238,39 +238,38 @@
 
     spatial.first_near()
     spatial.second_near(0)
+    scored.first_near()
     scored.second_near(0)
     spatial.first_far()
-    scored.first_near()
     spatial.second_near(1)
+    scored.first_far()
+    scored.lift(0)
+    spatial.second_near(2)
+    scored.lift(1)
+    spatial.second_far(0)
+    scored.lift(3)
+    scored.second_near(1)
     valued.own()
-    spatial.second_near(2)
-    scored.lift(3)
-    spatial.second_far(0)
     scored.lift(4)
-    scored.first_far()
+    scored.second_near(2)
     scored.second_far(0)
-    scored.lift(0)
+    scored.lift(2)
     valued.first_near()
+    scored.lift(5)
     spatial.second_near(3)
-    scored.lift(1)
-    scored.lift(2)
+    spatial.second_far(1)
+    scored.lift(6)
     valued.first_far()
-    scored.second_near(1)
-    scored.lift(11)
-    scored.second_near(2)
-    valued.lift(0)
-    spatial.second_far(1)
-    valued.lift(1)
-    valued.lift(2)
+    scored.second_near(3)
+    scored.lift(7)
     spatial.second_far(2)
-    scored.lift(5)
-    scored.second_near(3)
+    scored.second_far(1)
+    scored.lift(8)
     valued.second_near(0)
+    scored.second_far(2)
     valued.second_near(1)
-    scored.lift(6)
     valued.second_near(2)
     spatial.second_far(3)
-    scored.lift(7)
     valued.second_near(3)
     loads[6].wait()
     temporal.own()
@@ -313,11 +312,18 @@
     kept = pltpu.make_async_copy(normed_v.at[block(tm)], spread_v.at[tm], local_sem.at[13])
     kept.start()
 
+    scored.second_far(3)
+    valued.second_far(0)
+    valued.second_far(1)
+    valued.second_far(2)
+    valued.second_far(3)
+    scored.lift(11)
     scored.lift(9)
-    scored.second_far(1)
-    valued.second_far(0)
-    scored.lift(8)
-    scored.second_far(2)
+    scored.lift(10)
+    scored.lift(12)
+    valued.lift(0)
+    valued.lift(1)
+    valued.lift(2)
 
     rows = lax.broadcasted_iota(jnp.int32, (positions, TM), 0) // per
     cols16 = lax.broadcasted_iota(jnp.int32, (positions, TM), 1)
@@ -331,15 +337,11 @@
     allowed_v[...] = jnp.where(jnp.where(pos_r == pos_c, pairs, 0.0) > 0.5, 0.0, MASKED)
     number_slots(ids_v, gates_v, cols_v, slots_t, loads[8:10], clip, tm)
 
-    valued.second_far(3)
-    valued.second_far(2)
-    valued.lift(3)
-    scored.second_far(3)
-    scored.lift(10)
-    valued.second_far(1)
     temporal.first_near()
     temporal.second_near(0)
+    valued.lift(3)
     valued.lift(4)
+    scored.lift(13)
     valued.lift(5)
     valued.lift(6)
     valued.lift(7)
@@ -348,18 +350,16 @@
     valued.lift(9)
     temporal.second_near(1)
     valued.lift(10)
-    scored.lift(12)
+    scored.lift(14)
     valued.lift(11)
     temporal.second_near(2)
-    scored.lift(13)
+    valued.lift(12)
+    valued.lift(13)
     valued.lift(14)
-    valued.lift(13)
-    scored.lift(14)
-    valued.lift(12)
     temporal.second_far(0)
     temporal.lift(0)
+    temporal.lift(1)
     temporal.lift(3)
-    temporal.lift(1)
     temporal.lift(4)
 
     scored.pushed()

time: 173 us -> 173 us (level)
  no operation moved by 1% of the time
where the time goes in v7:
time: 173 us
  Pallas kernels  170 us (98%)
  local copies, waits for them, and re-layouts  2.3 us (1%)
    pallas_call x1, Pallas kernels, layer(): pl.pallas_call(layer_kernel, out_shape=jax.ShapeDtypeStruct((positions, m...  170 us

profile of v7, /device:TPU:1, one launch (start us, length us, event | category | flops | bytes accessed | tf_op | source)
XLA Modules:
  0.0 172.5 jit_solution(6245484362014448862)
XLA Ops:
  0.0 170.2 %layer.1 = bf16[256,2048]{1,0:T(8,128)(2,1)} custom-call(bf16[256,2048]{1,0:T(8,128)(2,1)} %bitcast.19, bf16[256,1024]{1,0:T(8,128)(2,1)} %bitcast.20, bf16[256,1024]{1,0:T(8,128)(2,1)} %bitcast.21, bf16[256,1024]{1,0:T(8,128)(2,1)} %bitcast.22, bf16[64,2048]{1,0:T(8,128)(2,1)} %sproj.1, bf16[128,3072]{1,0:T(8,128)(2,1)} %tqkv.1, bf16[64,2048]{1,0:T(8,128)(2,1)} %tproj.1, ...), custom_call_target="tpu_custom_call" | custom-call | tf_op jit(solution)/shard_map/layer/pallas_call | solution.py:648
  170.2 2.3 %copy.15 = bf16[1,1,256,2048]{3,2,1,0:T(8,128)(2,1)} copy(bf16[1,1,256,2048]{3,2,1,0:T(8,128)(2,1)} %bitcast.18) | data formatting | bytes 2097152
